TPU v7x, 256 devices: a whole 4x4x8 slice. The times are simulated.
256 devices in a mesh: row: 32 (over x_hi, z, core), col: 8 (over y, x_lo).
Axes of the slice: x: 4 (x_hi: 2, x_lo: 2; x = x_hi * 2 + x_lo), y: 4, z: 8, core: 2. Of those that a mesh axis runs over, the one named last changes fastest.
Arguments:
- seq_state: bfloat16 [2048, 1024], P('row'), may hold values from -6 to 6
- pair_state: bfloat16 [2048, 2048, 128], P('row', 'col'), may hold values from -8 to 8
- w_bias: bfloat16 [128, 32], replicated, may hold values from -12 to 12
- w_qkv: bfloat16 [3, 1024, 1024], P(None, None, 'col'), may hold values from -0.1875 to 0.1875
- w_gate: bfloat16 [1024, 1024], P(None, 'col'), may hold values from -0.1875 to 0.1875
- w_out: bfloat16 [1024, 1024], replicated, may hold values from -0.8984375 to 0.8984375
- w_seq_pair: bfloat16 [1024, 128], replicated, may hold values from -0.1875 to 0.1875
- w_pair_out: bfloat16 [128, 128], replicated, may hold values from -0.5 to 0.5
- w_up: bfloat16 [128, 512], replicated, may hold values from -0.5 to 0.5
- w_down: bfloat16 [512, 128], replicated, may hold values from -0.25 to 0.25
Outputs:
- seq_out: bfloat16 [2048, 1024], P('row')
- pair_out: bfloat16 [2048, 2048, 128], P('row', 'col')
All inputs are finite; a program needn't handle non-finite values.
Results may differ from a plain program's by a relative error of at most 0.018.
The roundings to bfloat16 on the way count: a program that leaves them out, or rounds other values in their place, can miss the bound.
Values may be sent and summed in bfloat16 or wider, within the bound.
A program may use at most 64 MiB of HBM per device.

v0:
```python
import math

import jax
import jax.numpy as jnp
from jax import lax
from jax.sharding import PartitionSpec as P

EPSILON = 1e-05


def sent_to_all(x, axis):
    peers = lax.axis_size(axis)
    return lax.all_to_all(jnp.broadcast_to(x[None], (peers, *x.shape)), axis, 0, 0, tiled=True)


def laid_out(pieces, dim):
    pieces = jnp.moveaxis(pieces, 0, dim)
    lengths = pieces.shape
    return pieces.reshape(*lengths[:dim], lengths[dim] * lengths[dim + 1], *lengths[dim + 2 :])


def collect(x, axis, dim):
    pieces = sent_to_all(x, axis)
    return laid_out(pieces, dim)


def layer_norm(values):
    centred = values - jnp.mean(values, axis=-1, keepdims=True)
    variance = jnp.mean(centred * centred, axis=-1, keepdims=True)
    return centred * lax.rsqrt(variance + EPSILON)


def body(seq_state, pair_state, w_bias, w_qkv, w_gate, w_out, w_seq_pair, w_pair_out, w_up, w_down):
    rows_here, model_width = seq_state.shape
    cols_here = pair_state.shape[1]
    channels = pair_state.shape[2]
    head_count = w_bias.shape[1]
    local_width = w_gate.shape[1]
    head_size = model_width // head_count
    local_heads = local_width // head_size
    pair_normed = layer_norm(pair_state.astype(jnp.float32)).astype(jnp.bfloat16)
    bias_local = jnp.einsum(
        "rcp,ph->hrc", pair_normed, w_bias, preferred_element_type=jnp.float32
    ).astype(jnp.bfloat16)
    bias_rows = lax.all_to_all(bias_local, "col", split_axis=0, concat_axis=2, tiled=True)
    normed = layer_norm(seq_state.astype(jnp.float32)).astype(jnp.bfloat16)
    queries = jnp.dot(normed, w_qkv[0], preferred_element_type=jnp.float32).astype(jnp.bfloat16)
    own_keys = jnp.dot(normed, w_qkv[1], preferred_element_type=jnp.float32).astype(jnp.bfloat16)
    own_values = jnp.dot(normed, w_qkv[2], preferred_element_type=jnp.float32).astype(jnp.bfloat16)
    key_value = collect(jnp.stack([own_keys, own_values]), "row", 1)
    length = key_value.shape[1]
    query_heads = queries.reshape(rows_here, local_heads, head_size)
    key_heads = key_value[0].reshape(length, local_heads, head_size)
    value_heads = key_value[1].reshape(length, local_heads, head_size)
    scale = 1.0 / math.sqrt(head_size)
    scores = jnp.einsum(
        "rhe,lhe->hrl", query_heads, key_heads, preferred_element_type=jnp.float32
    ) * scale + bias_rows.astype(jnp.float32)
    row_peak = jnp.max(scores, axis=-1, keepdims=True)
    weights = jnp.exp(scores - row_peak)
    probs = (weights / jnp.sum(weights, axis=-1, keepdims=True)).astype(jnp.bfloat16)
    mixed_heads = jnp.einsum(
        "hrl,lhe->rhe", probs, value_heads, preferred_element_type=jnp.float32
    ).reshape(rows_here, local_width)
    gate_values = jax.nn.sigmoid(jnp.dot(normed, w_gate, preferred_element_type=jnp.float32))
    attended = (mixed_heads * gate_values).astype(jnp.bfloat16)
    gathered = collect(attended, "col", 1)
    update_seq = jnp.dot(gathered, w_out, preferred_element_type=jnp.float32)
    seq_out = (seq_state.astype(jnp.float32) + update_seq).astype(jnp.bfloat16)
    new_normed = layer_norm(seq_out.astype(jnp.float32)).astype(jnp.bfloat16)
    inner_width = w_seq_pair.shape[1] // 2
    left_side = lax.optimization_barrier(
        jnp.dot(new_normed, w_seq_pair[:, :inner_width], preferred_element_type=jnp.float32).astype(
            jnp.bfloat16
        )
    ).astype(jnp.float32)
    right_side = jnp.einsum(
        "rd,di->ir", new_normed, w_seq_pair[:, inner_width:], preferred_element_type=jnp.float32
    ).astype(jnp.bfloat16)
    right_all = collect(right_side, "row", 1)
    right_cols = (
        lax.dynamic_slice_in_dim(right_all, lax.axis_index("col") * cols_here, cols_here, 1)
        .astype(jnp.float32)
        .T
    )
    block_size = math.gcd(rows_here, max(1, 4096 // cols_here))
    block_count = rows_here // block_size

    def pair_block(block_items):
        block_rows, left_rows = block_items
        product = left_rows[:, None, :] * right_cols[None, :, :]
        difference = left_rows[:, None, :] - right_cols[None, :, :]
        features = (
            jnp.concatenate([product, difference], axis=-1)
            .astype(jnp.bfloat16)
            .reshape(-1, 2 * inner_width)
        )
        updated = block_rows.astype(jnp.float32).reshape(-1, channels) + jnp.dot(
            features, w_pair_out, preferred_element_type=jnp.float32
        )
        hidden = jax.nn.relu(
            jnp.dot(
                layer_norm(updated).astype(jnp.bfloat16), w_up, preferred_element_type=jnp.float32
            )
        ).astype(jnp.bfloat16)
        result = updated + jnp.dot(hidden, w_down, preferred_element_type=jnp.float32)
        return result.astype(jnp.bfloat16).reshape(block_rows.shape)

    pair_out = lax.map(
        pair_block,
        (
            pair_state.reshape(block_count, block_size, cols_here, channels),
            left_side.reshape(block_count, block_size, inner_width),
        ),
    )
    return (seq_out, pair_out.reshape(rows_here, cols_here, channels))


def solution(mesh):
    return jax.shard_map(
        body,
        mesh=mesh,
        in_specs=(
            P("row", None),
            P("row", "col", None),
            P(),
            P(None, None, "col"),
            P(None, "col"),
            P(),
            P(),
            P(),
            P(),
            P(),
        ),
        out_specs=(P("row", None), P("row", "col", None)),
        check_vma=False,
    )
```

profile of v0, /device:TPU:1, one launch (start us, length us, event | category | flops | bytes accessed | tf_op | source)
XLA Modules:
  0.0 174.2 jit_solution(1289548785942187969)
XLA Ops:
  0.7 3.5 %convert_reduce_fusion = f32[64,256]{1,0:T(8,128)S(1)} fusion(bf16[64,256,128]{2,1,0:T(8,128)(2,1)} %param.13), kind=kLoop, calls=%fused_computation.22 | loop fusion | flops 4177920 | bytes 4259840 | tf_op jit(solution)/shard_map/reduce_sum | solution.py:28
  4.2 4.7 %fusion.13 = f32[64,256]{1,0:T(8,128)S(1)} fusion(bf16[64,256,128]{2,1,0:T(8,128)(2,1)S(1)} %copy-done.2, f32[64,256]{1,0:T(8,128)S(1)} %broadcast_multiply_fusion.1), kind=kLoop, calls=%fused_computation.25 | loop fusion | flops 8372224 | bytes 4325376 | tf_op jit(solution)/shard_map/reduce_sum | solution.py:29
  9.0 6.0 %fusion.25 = bf16[32,64,256]{2,0,1:T(8,128)(2,1)S(1)} fusion(bf16[64,256,128]{2,1,0:T(8,128)(2,1)S(1)} %copy-done.2, f32[64,256]{1,0:T(8,128)S(1)} %add_rsqrt_fusion.1, f32[64,256]{1,0:T(8,128)S(1)} %broadcast_multiply_fusion.1, bf16[128,32]{0,1:T(8,128)(2,1)S(1)} %copy-done.9), kind=kOutput, calls=%fused_computation.37 | convolution fusion | flops 143130624 | bytes 5382144 | tf_op jit(solution)/shard_map/rcp,ph->hrc/dot_general | solution.py:42
  16.6 5.9 %all-to-all-start.1 = ((bf16[32,64,256]{2,1,0:T(8,128)(2,1)}), bf16[32,64,256]{2,1,0:T(8,128)(2,1)S(1)}, u32[]{:S(2)}, u32[]{:S(2)}) async-start(bf16[32,64,256]{2,1,0:T(8,128)(2,1)} %copy.23), calls=%async_computation.1 | async-start | bytes 2097152 | tf_op jit(solution)/shard_map/all_to_all | solution.py:45
  25.3 11.8 %all-to-all-done.1 = bf16[32,64,256]{2,1,0:T(8,128)(2,1)S(1)} async-done(((bf16[32,64,256]{2,1,0:T(8,128)(2,1)}), bf16[32,64,256]{2,1,0:T(8,128)(2,1)S(1)}, u32[]{:S(2)}, u32[]{:S(2)}) %all-to-all-start.1) | async-done | bytes 1048608 | tf_op jit(solution)/shard_map/all_to_all | solution.py:45
  38.3 12.9 %all-to-all-start = ((bf16[32,2,64,128]{3,2,1,0:T(8,128)(2,1)}), bf16[32,2,64,128]{3,2,1,0:T(8,128)(2,1)}, u32[]{:S(2)}, u32[]{:S(2)}) async-start(bf16[32,2,64,128]{3,2,1,0:T(8,128)(2,1)} %broadcast_in_dim.11), calls=%async_computation | async-start | bytes 2097152 | tf_op jit(solution)/shard_map/all_to_all | solution.py:13
  52.6 1.9 %copy.35 = f32[8,4,64,256]{3,0,2,1:T(8,128)} copy(bf16[8,4,64,256]{3,2,1,0:T(8,128)(2,1)S(1)} %bitcast.101) | data formatting | bytes 3145728 | tf_op jit(solution)/shard_map/convert_element_type | solution.py:58
  54.5 2.7 %reshape.119 = f32[4,64,2048]{2,1,0:T(8,128)} reshape(f32[4,64,8,256]{3,2,1,0:T(8,128)} %bitcast.100) | data formatting | bytes 4194304 | tf_op jit(solution)/shard_map/convert_element_type | solution.py:58
  57.2 21.4 %all-to-all-done = bf16[32,2,64,128]{3,2,1,0:T(8,128)(2,1)} async-done(((bf16[32,2,64,128]{3,2,1,0:T(8,128)(2,1)}), bf16[32,2,64,128]{3,2,1,0:T(8,128)(2,1)}, u32[]{:S(2)}, u32[]{:S(2)}) %all-to-all-start) | async-done | bytes 1048608 | tf_op jit(solution)/shard_map/all_to_all | solution.py:13
  78.7 2.2 %fusion.65 = (bf16[1,32,64,128]{3,2,0,1:T(8,128)(2,1)}, bf16[1,32,64,128]{3,2,0,1:T(8,128)(2,1)}) fusion(bf16[2,32,64,128]{3,2,0,1:T(8,128)(2,1)} %bitcast.9), kind=kLoop, calls=%fused_computation.88 | loop fusion | bytes 2097152 | tf_op jit(solution)/shard_map/slice | solution.py:53
  80.9 2.5 %copy.22 = bf16[1,32,64,128]{2,1,3,0:T(8,128)(2,1)S(1)} copy(bf16[1,32,64,128]{3,2,0,1:T(8,128)(2,1)} %get-tuple-element.65) | data formatting | bytes 1048576 | tf_op jit(solution)/shard_map/slice | solution.py:53
  83.4 1.6 reshape_squeeze.7
  85.0 2.2 %fusion.21 = f32[4,64,2048]{2,1,0:T(8,128)S(1)} fusion(f32[4,64,2048]{2,1,0:T(8,128)} %reshape.119, bf16[64,4,32]{0,2,1:T(8,128)(2,1)S(1)} %bitcast.103, bf16[2048,4,32]{0,2,1:T(8,128)(2,1)} %reshape_squeeze.7), kind=kOutput, calls=%fused_computation.33 | convolution fusion | flops 34603008 | bytes 4734976 | tf_op jit(solution)/shard_map/rhe,lhe->hrl/dot_general | solution.py:56
  89.0 2.5 %copy.20 = bf16[1,32,64,128]{2,1,3,0:T(8,128)(2,1)S(1)} copy(bf16[1,32,64,128]{3,2,0,1:T(8,128)(2,1)} %get-tuple-element.66) | data formatting | bytes 1048576 | tf_op jit(solution)/shard_map/slice | solution.py:54
  91.5 1.6 reshape_squeeze.6
  93.1 3.0 %fusion.37 = f32[4,32,64]{2,1,0:T(8,128)S(1)} fusion(bf16[2048,4,32]{0,2,1:T(8,128)(2,1)} %reshape_squeeze.6, f32[4,64]{1,0:T(4,128)S(1)} %fusion.66, f32[4,64,2048]{2,1,0:T(8,128)} %copy-done.3), kind=kOutput, calls=%fused_computation.54 | convolution fusion | flops 35129600 | bytes 2655232 | tf_op jit(solution)/shard_map/hrl,lhe->rhe/dot_general | solution.py:62
  96.5 7.9 %all_to_all.24 = bf16[8,64,128]{2,1,0:T(8,128)(2,1)S(1)} all-to-all(bf16[8,64,128]{2,1,0:T(8,128)(2,1)S(1)} %broadcast_in_dim.12), channel_id=1, replica_groups=mesh['row'=32,'col'=8] {'col'}, dimensions={0} | all-to-all | bytes 262144 | tf_op jit(solution)/shard_map/all_to_all | solution.py:13
  106.8 7.8 %all-to-all-start.3 = ((bf16[32,2,2048]{2,1,0:T(2,128)(2,1)}), bf16[32,2,2048]{2,1,0:T(2,128)(2,1)S(1)}, u32[]{:S(2)}, u32[]{:S(2)}) async-start(bf16[32,2,2048]{2,1,0:T(2,128)(2,1)} %reshape.124), calls=%async_computation.3 | async-start | bytes 524288 | tf_op jit(solution)/shard_map/all_to_all | solution.py:13
  114.8 12.8 %all-to-all-done.3 = bf16[32,2,2048]{2,1,0:T(2,128)(2,1)S(1)} async-done(((bf16[32,2,2048]{2,1,0:T(2,128)(2,1)}), bf16[32,2,2048]{2,1,0:T(2,128)(2,1)S(1)}, u32[]{:S(2)}, u32[]{:S(2)}) %all-to-all-start.3) | async-done | bytes 262176 | tf_op jit(solution)/shard_map/all_to_all | solution.py:13
  128.0 46.2 %while.10 = (s32[]{:T(128)}, bf16[4,16,256,128]{3,2,1,0:T(8,128)(2,1)}, bf16[4,16,256,128]{3,2,1,0:T(8,128)(2,1)}, f32[4,16,64]{2,1,0:T(8,128)S(1)}, f32[256,64]...) while((s32[]{:T(128)}, ...), condition=%wide.region_11.12_spmd, body=%wide.region_8.11_spmd.sunk | while | flops 1221070848 | bytes 23589504 | solution.py:109
  133.7 4.8 %fusion.87 = bf16[4096,128]{1,0:T(8,128)(2,1)S(1)} fusion(f32[4096,128]{1,0:T(8,128)} %copy-done.1, bf16[512,128]{1,0:T(8,128)(2,1)} %get-tuple-element.151, bf16[128,512]{1,0:T(8,128)(2,1)} %get-tuple-element.150, f32[4096]{0:T(1024)S(1)} %add_rsqrt_fusion.5, f32[4096]{0:T(1024)S(1)} %broadcast_multiply_fusion.5), kind=kOutput, calls=%fused_computation.3.clone.1 | convolution fusion | flops 1080557568 | bytes 3440640 | tf_op jit(solution)/shard_map/while/body/eval_jaxpr/dot_general | solution.py:106
  145.2 4.9 %fusion.87 = bf16[4096,128]{1,0:T(8,128)(2,1)S(1)} fusion(f32[4096,128]{1,0:T(8,128)} %copy-done.1, bf16[512,128]{1,0:T(8,128)(2,1)} %get-tuple-element.151, bf16[128,512]{1,0:T(8,128)(2,1)} %get-tuple-element.150, f32[4096]{0:T(1024)S(1)} %add_rsqrt_fusion.5, f32[4096]{0:T(1024)S(1)} %broadcast_multiply_fusion.5), kind=kOutput, calls=%fused_computation.3.clone.1 | convolution fusion | flops 1080557568 | bytes 3440640 | tf_op jit(solution)/shard_map/while/body/eval_jaxpr/dot_general | solution.py:106
  156.7 4.8 %fusion.87 = bf16[4096,128]{1,0:T(8,128)(2,1)S(1)} fusion(f32[4096,128]{1,0:T(8,128)} %copy-done.1, bf16[512,128]{1,0:T(8,128)(2,1)} %get-tuple-element.151, bf16[128,512]{1,0:T(8,128)(2,1)} %get-tuple-element.150, f32[4096]{0:T(1024)S(1)} %add_rsqrt_fusion.5, f32[4096]{0:T(1024)S(1)} %broadcast_multiply_fusion.5), kind=kOutput, calls=%fused_computation.3.clone.1 | convolution fusion | flops 1080557568 | bytes 3440640 | tf_op jit(solution)/shard_map/while/body/eval_jaxpr/dot_general | solution.py:106
  168.3 4.9 %fusion.87 = bf16[4096,128]{1,0:T(8,128)(2,1)S(1)} fusion(f32[4096,128]{1,0:T(8,128)} %copy-done.1, bf16[512,128]{1,0:T(8,128)(2,1)} %get-tuple-element.151, bf16[128,512]{1,0:T(8,128)(2,1)} %get-tuple-element.150, f32[4096]{0:T(1024)S(1)} %add_rsqrt_fusion.5, f32[4096]{0:T(1024)S(1)} %broadcast_multiply_fusion.5), kind=kOutput, calls=%fused_computation.3.clone.1 | convolution fusion | flops 1080557568 | bytes 3440640 | tf_op jit(solution)/shard_map/while/body/eval_jaxpr/dot_general | solution.py:106
  (87 shorter events, 38.4 us)
Async XLA Ops:
  0.6 103.8 %copy-start = (bf16[1024,1024]{1,0:T(8,128)(2,1)S(1)}, bf16[1024,1024]{1,0:T(8,128)(2,1)}, u32[]{:S(2)}) copy-start(bf16[1024,1024]{1,0:T(8,128)(2,1)} %param.17) | copy-start | bytes 6291460
  0.6 3.6 %copy-start.2 = (bf16[64,256,128]{2,1,0:T(8,128)(2,1)S(1)}, bf16[64,256,128]{2,1,0:T(8,128)(2,1)}, u32[]{:S(2)}) copy-start(bf16[64,256,128]{2,1,0:T(8,128)(2,1)} %param.13) | copy-start | bytes 12582916
  4.2 4.8 %copy-start.9 = (bf16[128,32]{0,1:T(8,128)(2,1)S(1)}, bf16[128,32]{0,1:T(8,128)(2,1)}, u32[]{:S(2)}) copy-start(bf16[128,32]{0,1:T(8,128)(2,1)} %param.14) | copy-start | bytes 24580
  15.0 7.5 %copy-start.4 = (bf16[64,1024]{1,0:T(8,128)(2,1)S(1)}, bf16[64,1024]{1,0:T(8,128)(2,1)}, u32[]{:S(2)}) copy-start(bf16[64,1024]{1,0:T(8,128)(2,1)} %param.12) | copy-start | bytes 393220
  16.6 20.5 %all-to-all-start.1 = ((bf16[32,64,256]{2,1,0:T(8,128)(2,1)}), bf16[32,64,256]{2,1,0:T(8,128)(2,1)S(1)}, u32[]{:S(2)}, u32[]{:S(2)}) async-start(bf16[32,64,256]{2,1,0:T(8,128)(2,1)} %copy.23), calls=%async_computation.1 | async-start | bytes 2097152 | tf_op jit(solution)/shard_map/all_to_all | solution.py:45
  38.3 40.4 %all-to-all-start = ((bf16[32,2,64,128]{3,2,1,0:T(8,128)(2,1)}), bf16[32,2,64,128]{3,2,1,0:T(8,128)(2,1)}, u32[]{:S(2)}, u32[]{:S(2)}) async-start(bf16[32,2,64,128]{3,2,1,0:T(8,128)(2,1)} %broadcast_in_dim.11), calls=%async_computation | async-start | bytes 2097152 | tf_op jit(solution)/shard_map/all_to_all | solution.py:13
  87.2 1.3 copy-start.3
  93.1 3.1 %copy-start.7 = (bf16[1024,128]{1,0:T(8,128)(2,1)S(1)}, bf16[1024,128]{1,0:T(8,128)(2,1)}, u32[]{:S(2)}) copy-start(bf16[1024,128]{1,0:T(8,128)(2,1)} %param.16) | copy-start | bytes 786436
  96.1 9.1 %copy-start.8 = (bf16[1024,128]{1,0:T(8,128)(2,1)S(1)}, bf16[1024,128]{1,0:T(8,128)(2,1)}, u32[]{:S(2)}) copy-start(bf16[1024,128]{1,0:T(8,128)(2,1)} %param.18) | copy-start | bytes 786436
  105.0 23.0 %copy-start.6 = (bf16[64,1024]{1,0:T(8,128)(2,1)}, bf16[64,1024]{1,0:T(8,128)(2,1)S(1)}, u32[]{:S(2)}) copy-start(bf16[64,1024]{1,0:T(8,128)(2,1)S(1)} %get-tuple-element.68) | copy-start | bytes 393220
  105.0 23.0 %copy-start.5 = (bf16[128,128]{1,0:T(8,128)(2,1)S(1)}, bf16[128,128]{1,0:T(8,128)(2,1)}, u32[]{:S(2)}) copy-start(bf16[128,128]{1,0:T(8,128)(2,1)} %param.19) | copy-start | bytes 98308
  106.8 20.9 %all-to-all-start.3 = ((bf16[32,2,2048]{2,1,0:T(2,128)(2,1)}), bf16[32,2,2048]{2,1,0:T(2,128)(2,1)S(1)}, u32[]{:S(2)}, u32[]{:S(2)}) async-start(bf16[32,2,2048]{2,1,0:T(2,128)(2,1)} %reshape.124), calls=%async_computation.3 | async-start | bytes 524288 | tf_op jit(solution)/shard_map/all_to_all | solution.py:13
  131.0 1.4 copy-start.1
  142.5 1.4 copy-start.1
  154.1 1.4 copy-start.1
  165.6 1.4 copy-start.1
where the time goes:
time: 175 us; the launch traced here: 174 us
  waiting for transfers between devices  46 us (26%)
  matrix products  40.1 us (23%)
  local copies, waits for them, and re-layouts  35.7 us (20%)
  starting transfers between devices  26.7 us (15%)
  other arithmetic  16.5 us (9%)
  blocking collectives  7.94 us (5%)
    all_to_all x2, waiting for transfers between devices, sent_to_all(): lax.all_to_all(jnp.broadcast_to(x[None], (peers, *x.shape)), axis, 0, 0,...  34.2 us
    all_to_all x2, starting transfers between devices, sent_to_all(): lax.all_to_all(jnp.broadcast_to(x[None], (peers, *x.shape)), axis, 0, 0,...  20.7 us
    dot_general x4, matrix products, pair_block(): jnp.dot(hidden, w_down, preferred_element_type=jnp.float32)  19.4 us
    all_to_all x1, waiting for transfers between devices, body(): lax.all_to_all(bias_local, 'col', split_axis=0, concat_axis=2, tiled=True)  11.8 us
    reduce_sum x7, other arithmetic, layer_norm(): variance = jnp.mean(centred * centred, axis=-1, keepdims=True)  10.3 us
    all_to_all x1, blocking collectives, sent_to_all(): lax.all_to_all(jnp.broadcast_to(x[None], (peers, *x.shape)), axis, 0, 0,...  7.94 us
    dot_general x1, matrix products, body(): jnp.einsum('rcp,ph->hrc', pair_normed, w_bias, preferred_element_type=jnp...  5.97 us
    all_to_all x1, starting transfers between devices, body(): lax.all_to_all(bias_local, 'col', split_axis=0, concat_axis=2, tiled=True)  5.94 us
  transfers between devices with their start and end apart: 3, of which 3 were waited for; matrix products, arithmetic and copies ran while one was open for 5% of the time, Pallas kernels for 0%

commit v1 on v0

--- a/solution.py
+++ b/solution.py
@@ -3,9 +3,82 @@
 import jax
 import jax.numpy as jnp
 from jax import lax
+from jax.experimental import pallas as pl
+from jax.experimental.pallas import tpu as pltpu
 from jax.sharding import PartitionSpec as P
 
 EPSILON = 1e-05
+
+F32 = jnp.float32
+BF16 = jnp.bfloat16
+PAIR_ROWS = 16
+PAIR_CHUNK = 4
+
+
+def dot32(a, b):
+    return jnp.dot(a, b, preferred_element_type=F32)
+
+
+def pair_kernel(x_ref, left_ref, right_ref, wp_ref, wu_ref, wd_ref, o_ref, mix_ref, right2_ref):
+    @pl.when(pl.program_id(0) == 0)
+    def _():
+        w = wp_ref[...].astype(F32)
+        centred = w - jnp.mean(w, axis=1, keepdims=True)
+        a = lax.broadcasted_iota(jnp.int32, (128, 128), 0)
+        b = lax.broadcasted_iota(jnp.int32, (128, 128), 1)
+        eye = jnp.where(a == b, 1.0, 0.0)
+        mix_ref[0:128, 0:128] = (eye - 1.0 / 128).astype(BF16)
+        mix_ref[0:128, 128:256] = eye.astype(BF16)
+        mix_ref[128:256, 0:128] = centred.astype(BF16)
+        mix_ref[128:256, 128:256] = wp_ref[...]
+        r = right_ref[...].astype(F32)
+        right2_ref[...] = jnp.concatenate([r, r], axis=1)
+
+    lane = lax.broadcasted_iota(jnp.int32, (1, 128), 1)
+    for start in range(0, PAIR_ROWS, PAIR_CHUNK):
+        features, rows = [], []
+        for i in range(start, start + PAIR_CHUNK):
+            left = left_ref[pl.ds(i, 1), :].astype(F32)
+            left2 = jnp.concatenate([left, left], axis=1)
+            scale = jnp.where(lane < 64, left2, -1.0)
+            shift = jnp.where(lane < 64, 0.0, left2)
+            features.append((right2_ref[...] * scale + shift).astype(BF16))
+            rows.append(x_ref[i])
+        mixed = dot32(
+            jnp.concatenate([jnp.concatenate(rows, axis=0), jnp.concatenate(features, axis=0)], axis=1),
+            mix_ref[...],
+        )
+        centred, updated = mixed[:, :128], mixed[:, 128:]
+        variance = jnp.mean(centred * centred, axis=1, keepdims=True)
+        normed = (centred * lax.rsqrt(variance + EPSILON)).astype(BF16)
+        hidden = jnp.maximum(dot32(normed, wu_ref[...]), 0.0).astype(BF16)
+        result = (updated + dot32(hidden, wd_ref[...])).astype(BF16)
+        for i in range(PAIR_CHUNK):
+            o_ref[start + i] = result[i * 256 : (i + 1) * 256]
+
+
+def pair_transition(x, left, right, wp, wu, wd):
+    rows = x.shape[0]
+
+    def whole(array):
+        return pl.BlockSpec(array.shape, lambda i: (0,) * array.ndim)
+
+    return pl.pallas_call(
+        pair_kernel,
+        grid=(rows // PAIR_ROWS,),
+        out_shape=jax.ShapeDtypeStruct(x.shape, BF16),
+        in_specs=[
+            pl.BlockSpec((PAIR_ROWS, 256, 128), lambda i: (i, 0, 0)),
+            pl.BlockSpec((PAIR_ROWS, 64), lambda i: (i, 0)),
+            whole(right),
+            whole(wp),
+            whole(wu),
+            whole(wd),
+        ],
+        out_specs=pl.BlockSpec((PAIR_ROWS, 256, 128), lambda i: (i, 0, 0)),
+        scratch_shapes=[pltpu.VMEM((256, 256), BF16), pltpu.VMEM((256, 128), F32)],
+        compiler_params=pltpu.CompilerParams(dimension_semantics=("arbitrary",)),
+    )(x, left, right, wp, wu, wd)
 
 
 def sent_to_all(x, axis):
@@ -73,47 +146,17 @@
         jnp.dot(new_normed, w_seq_pair[:, :inner_width], preferred_element_type=jnp.float32).astype(
             jnp.bfloat16
         )
-    ).astype(jnp.float32)
+    )
     right_side = jnp.einsum(
         "rd,di->ir", new_normed, w_seq_pair[:, inner_width:], preferred_element_type=jnp.float32
     ).astype(jnp.bfloat16)
     right_all = collect(right_side, "row", 1)
     right_cols = (
         lax.dynamic_slice_in_dim(right_all, lax.axis_index("col") * cols_here, cols_here, 1)
-        .astype(jnp.float32)
         .T
     )
-    block_size = math.gcd(rows_here, max(1, 4096 // cols_here))
-    block_count = rows_here // block_size
-
-    def pair_block(block_items):
-        block_rows, left_rows = block_items
-        product = left_rows[:, None, :] * right_cols[None, :, :]
-        difference = left_rows[:, None, :] - right_cols[None, :, :]
-        features = (
-            jnp.concatenate([product, difference], axis=-1)
-            .astype(jnp.bfloat16)
-            .reshape(-1, 2 * inner_width)
-        )
-        updated = block_rows.astype(jnp.float32).reshape(-1, channels) + jnp.dot(
-            features, w_pair_out, preferred_element_type=jnp.float32
-        )
-        hidden = jax.nn.relu(
-            jnp.dot(
-                layer_norm(updated).astype(jnp.bfloat16), w_up, preferred_element_type=jnp.float32
-            )
-        ).astype(jnp.bfloat16)
-        result = updated + jnp.dot(hidden, w_down, preferred_element_type=jnp.float32)
-        return result.astype(jnp.bfloat16).reshape(block_rows.shape)
-
-    pair_out = lax.map(
-        pair_block,
-        (
-            pair_state.reshape(block_count, block_size, cols_here, channels),
-            left_side.reshape(block_count, block_size, inner_width),
-        ),
-    )
-    return (seq_out, pair_out.reshape(rows_here, cols_here, channels))
+    pair_out = pair_transition(pair_state, left_side, right_cols, w_pair_out, w_up, w_down)
+    return (seq_out, pair_out)
 
 
 def solution(mesh):

time: 175 us -> 145 us (0.83)
  matrix products: 40.1 us -> 16.6 us
  Pallas kernels: 0 us -> 15 us
  local copies, waits for them, and re-layouts: 35.7 us -> 22.2 us
  other arithmetic: 16.5 us -> 9.29 us
    dot_general x8 -> x0, matrix products: 24 us -> none  [the longest x4 19.4 us: pair_block(): jnp.dot(hidden, w_down, preferred_element_type=jnp.float32)]
    pallas_call x0 -> x1, Pallas kernels: none -> 15 us  [pair_transition(): pl.pallas_call(pair_kernel, grid=(rows // PAIR_ROWS,), out_shape=jax.Shap...]
    while x8 -> x0, local copies, waits for them, and re-layouts: 5.33 us -> none
    dynamic_slice x4 -> x0, local copies, waits for them, and re-layouts: 5.2 us -> none  [body(): lax.map(pair_block, (pair_state.reshape(block_count, block_size, cols_her...]
    reduce_sum x7 -> x3, other arithmetic: 10.3 us -> 5.13 us  [layer_norm(): variance = jnp.mean(centred * centred, axis=-1, keepdims=True)]
    dynamic_update_slice x4 -> x0, local copies, waits for them, and re-layouts: 4.2 us -> none  [body(): lax.map(pair_block, (pair_state.reshape(block_count, block_size, cols_her...]
    another operation x4 -> x0, other arithmetic: 1.95 us -> none
    unnamed x21 -> x23, local copies, waits for them, and re-layouts: 2.98 us -> 3.57 us
  transfers between devices with their start and end apart: 3 -> 3, of which waited for: 3 -> 3; matrix products, arithmetic and copies ran while one was open for 5% -> 7% of each run, Pallas kernels for 0% -> 0%
where the time goes in v1:
time: 145 us; the launch traced here: 144 us
  waiting for transfers between devices  45.4 us (31%)
  starting transfers between devices  26.7 us (18%)
  local copies, waits for them, and re-layouts  22.2 us (15%)
  matrix products  16.6 us (11%)
  Pallas kernels  15 us (10%)
  other arithmetic  9.29 us (6%)
  blocking collectives  7.94 us (5%)
    all_to_all x2, waiting for transfers between devices, sent_to_all(): lax.all_to_all(jnp.broadcast_to(x[None], (peers, *x.shape)), axis, 0, 0,...  33.6 us
    all_to_all x2, starting transfers between devices, sent_to_all(): lax.all_to_all(jnp.broadcast_to(x[None], (peers, *x.shape)), axis, 0, 0,...  20.7 us
    pallas_call x1, Pallas kernels, pair_transition(): pl.pallas_call(pair_kernel, grid=(rows // PAIR_ROWS,), out_shape=jax.Shap...  15 us
    all_to_all x1, waiting for transfers between devices, body(): lax.all_to_all(bias_local, 'col', split_axis=0, concat_axis=2, tiled=True)  11.8 us
    all_to_all x1, blocking collectives, sent_to_all(): lax.all_to_all(jnp.broadcast_to(x[None], (peers, *x.shape)), axis, 0, 0,...  7.94 us
    dot_general x1, matrix products, body(): jnp.einsum('rcp,ph->hrc', pair_normed, w_bias, preferred_element_type=jnp...  5.97 us
    all_to_all x1, starting transfers between devices, body(): lax.all_to_all(bias_local, 'col', split_axis=0, concat_axis=2, tiled=True)  5.94 us
    reduce_sum x3, other arithmetic, layer_norm(): variance = jnp.mean(centred * centred, axis=-1, keepdims=True)  5.13 us
  transfers between devices with their start and end apart: 3, of which 3 were waited for; matrix products, arithmetic and copies ran while one was open for 7% of the time, Pallas kernels for 0%

profile of v1, /device:TPU:1, one launch (start us, length us, event | category | flops | bytes accessed | tf_op | source)
XLA Modules:
  0.0 144.1 jit_solution(17532705862511948842)
XLA Ops:
  0.7 3.5 %convert_reduce_fusion = f32[64,256]{1,0:T(8,128)S(1)} fusion(bf16[64,256,128]{2,1,0:T(8,128)(2,1)} %x_ref.1), kind=kLoop, calls=%fused_computation.2 | loop fusion | flops 4177920 | bytes 4259840 | tf_op jit(solution)/shard_map/reduce_sum | solution.py:101
  4.2 4.7 %fusion.3 = f32[64,256]{1,0:T(8,128)S(1)} fusion(bf16[64,256,128]{2,1,0:T(8,128)(2,1)S(1)} %copy-done.1, f32[64,256]{1,0:T(8,128)S(1)} %broadcast_multiply_fusion), kind=kLoop, calls=%fused_computation.5 | loop fusion | flops 8372224 | bytes 4325376 | tf_op jit(solution)/shard_map/reduce_sum | solution.py:102
  9.0 6.0 %fusion.15 = bf16[32,64,256]{2,0,1:T(8,128)(2,1)S(1)} fusion(bf16[64,256,128]{2,1,0:T(8,128)(2,1)S(1)} %copy-done.1, f32[64,256]{1,0:T(8,128)S(1)} %add_rsqrt_fusion, f32[64,256]{1,0:T(8,128)S(1)} %broadcast_multiply_fusion, bf16[128,32]{0,1:T(8,128)(2,1)S(1)} %copy-done.9), kind=kOutput, calls=%fused_computation.17 | convolution fusion | flops 143130624 | bytes 5382144 | tf_op jit(solution)/shard_map/rcp,ph->hrc/dot_general | solution.py:115
  15.0 1.6 %copy.23 = bf16[32,64,256]{2,1,0:T(8,128)(2,1)} copy(bf16[32,64,256]{2,0,1:T(8,128)(2,1)S(1)} %fusion.15) | data formatting | bytes 2097152 | tf_op jit(solution)/shard_map/convert_element_type | solution.py:117
  16.6 5.9 %all-to-all-start.1 = ((bf16[32,64,256]{2,1,0:T(8,128)(2,1)}), bf16[32,64,256]{2,1,0:T(8,128)(2,1)S(1)}, u32[]{:S(2)}, u32[]{:S(2)}) async-start(bf16[32,64,256]{2,1,0:T(8,128)(2,1)} %copy.23), calls=%async_computation.1 | async-start | bytes 2097152 | tf_op jit(solution)/shard_map/all_to_all | solution.py:118
  22.9 1.2 fusion.25
  25.3 11.8 %all-to-all-done.1 = bf16[32,64,256]{2,1,0:T(8,128)(2,1)S(1)} async-done(((bf16[32,64,256]{2,1,0:T(8,128)(2,1)}), bf16[32,64,256]{2,1,0:T(8,128)(2,1)S(1)}, u32[]{:S(2)}, u32[]{:S(2)}) %all-to-all-start.1) | async-done | bytes 1048608 | tf_op jit(solution)/shard_map/all_to_all | solution.py:118
  37.1 1.2 broadcast_in_dim.6
  38.3 12.9 %all-to-all-start = ((bf16[32,2,64,128]{3,2,1,0:T(8,128)(2,1)}), bf16[32,2,64,128]{3,2,1,0:T(8,128)(2,1)}, u32[]{:S(2)}, u32[]{:S(2)}) async-start(bf16[32,2,64,128]{3,2,1,0:T(8,128)(2,1)} %broadcast_in_dim.6), calls=%async_computation | async-start | bytes 2097152 | tf_op jit(solution)/shard_map/all_to_all | solution.py:86
  52.6 1.9 %copy.35 = f32[8,4,64,256]{3,0,2,1:T(8,128)} copy(bf16[8,4,64,256]{3,2,1,0:T(8,128)(2,1)S(1)} %bitcast.66) | data formatting | bytes 3145728 | tf_op jit(solution)/shard_map/convert_element_type | solution.py:131
  54.5 2.7 %reshape.70 = f32[4,64,2048]{2,1,0:T(8,128)} reshape(f32[4,64,8,256]{3,2,1,0:T(8,128)} %bitcast.65) | data formatting | bytes 4194304 | tf_op jit(solution)/shard_map/convert_element_type | solution.py:131
  57.2 21.4 %all-to-all-done = bf16[32,2,64,128]{3,2,1,0:T(8,128)(2,1)} async-done(((bf16[32,2,64,128]{3,2,1,0:T(8,128)(2,1)}), bf16[32,2,64,128]{3,2,1,0:T(8,128)(2,1)}, u32[]{:S(2)}, u32[]{:S(2)}) %all-to-all-start) | async-done | bytes 1048608 | tf_op jit(solution)/shard_map/all_to_all | solution.py:86
  78.7 2.2 %fusion.54 = (bf16[1,32,64,128]{3,2,0,1:T(8,128)(2,1)}, bf16[1,32,64,128]{3,2,0,1:T(8,128)(2,1)}) fusion(bf16[2,32,64,128]{3,2,0,1:T(8,128)(2,1)} %bitcast.4), kind=kLoop, calls=%fused_computation.67 | loop fusion | bytes 2097152 | tf_op jit(solution)/shard_map/slice | solution.py:126
  80.9 2.5 %copy.20 = bf16[1,32,64,128]{2,1,3,0:T(8,128)(2,1)S(1)} copy(bf16[1,32,64,128]{3,2,0,1:T(8,128)(2,1)} %get-tuple-element.3) | data formatting | bytes 1048576 | tf_op jit(solution)/shard_map/slice | solution.py:127
  83.4 1.6 %reshape_squeeze.6 = bf16[2048,4,32]{0,2,1:T(8,128)(2,1)} reshape(bf16[1,32,64,128]{2,1,3,0:T(8,128)(2,1)S(1)} %copy.20) | data formatting | bytes 1048576 | tf_op jit(solution)/shard_map/reshape;squeeze | solution.py:127
  85.0 2.5 %copy.22 = bf16[1,32,64,128]{2,1,3,0:T(8,128)(2,1)S(1)} copy(bf16[1,32,64,128]{3,2,0,1:T(8,128)(2,1)} %get-tuple-element.2) | data formatting | bytes 1048576 | tf_op jit(solution)/shard_map/slice | solution.py:126
  87.4 1.6 %reshape_squeeze.7 = bf16[2048,4,32]{0,2,1:T(8,128)(2,1)} reshape(bf16[1,32,64,128]{2,1,3,0:T(8,128)(2,1)S(1)} %copy.22) | data formatting | bytes 1048576 | tf_op jit(solution)/shard_map/reshape;squeeze | solution.py:126
  89.0 2.2 %fusion.11 = f32[4,64,2048]{2,1,0:T(8,128)S(1)} fusion(f32[4,64,2048]{2,1,0:T(8,128)} %reshape.70, bf16[64,4,32]{0,2,1:T(8,128)(2,1)S(1)} %bitcast.68, bf16[2048,4,32]{0,2,1:T(8,128)(2,1)} %reshape_squeeze.7), kind=kOutput, calls=%fused_computation.13 | convolution fusion | flops 34603008 | bytes 4734976 | tf_op jit(solution)/shard_map/rhe,lhe->hrl/dot_general | solution.py:129
  91.3 1.3 copy-done.2
  93.7 2.9 %fusion.27 = f32[4,32,64]{2,1,0:T(8,128)S(1)} fusion(bf16[2048,4,32]{0,2,1:T(8,128)(2,1)S(1)} %copy-done.4, f32[4,64]{1,0:T(4,128)S(1)} %fusion.55, f32[4,64,2048]{2,1,0:T(8,128)} %copy-done.2), kind=kOutput, calls=%fused_computation.34 | convolution fusion | flops 35129600 | bytes 2655232 | tf_op jit(solution)/shard_map/hrl,lhe->rhe/dot_general | solution.py:135
  96.9 7.9 %all_to_all.24 = bf16[8,64,128]{2,1,0:T(8,128)(2,1)S(1)} all-to-all(bf16[8,64,128]{2,1,0:T(8,128)(2,1)S(1)} %broadcast_in_dim.7), channel_id=1, replica_groups=mesh['row'=32,'col'=8] {'col'}, dimensions={0} | all-to-all | bytes 262144 | tf_op jit(solution)/shard_map/all_to_all | solution.py:86
  107.2 7.8 %all-to-all-start.3 = ((bf16[32,2,2048]{2,1,0:T(2,128)(2,1)}), bf16[32,2,2048]{2,1,0:T(2,128)(2,1)S(1)}, u32[]{:S(2)}, u32[]{:S(2)}) async-start(bf16[32,2,2048]{2,1,0:T(2,128)(2,1)} %reshape.73), calls=%async_computation.3 | async-start | bytes 524288 | tf_op jit(solution)/shard_map/all_to_all | solution.py:86
  115.9 12.2 %all-to-all-done.3 = bf16[32,2,2048]{2,1,0:T(2,128)(2,1)S(1)} async-done(((bf16[32,2,2048]{2,1,0:T(2,128)(2,1)}), bf16[32,2,2048]{2,1,0:T(2,128)(2,1)S(1)}, u32[]{:S(2)}, u32[]{:S(2)}) %all-to-all-start.3) | async-done | bytes 262176 | tf_op jit(solution)/shard_map/all_to_all | solution.py:86
  129.1 15.0 %shard_map.113 = bf16[64,256,128]{2,1,0:T(8,128)(2,1)} custom-call(bf16[64,256,128]{2,1,0:T(8,128)(2,1)} %x_ref.1, bf16[64,64]{1,0:T(8,128)(2,1)} %convolution_convert_fusion.1.left_ref, bf16[256,64]{1,0:T(8,128)(2,1)} %dynamic-slice_bitcast_fusion.right_ref, bf16[128,128]{1,0:T(8,128)(2,1)} %wp_ref.1, bf16[128,512]{1,0:T(8,128)(2,1)} %wu_ref.1, ...), custom_call_target="tpu_custom_call" | custom-call | tf_op jit(solution)/shard_map/pallas_call | solution.py:66
  (43 shorter events, 8.4 us)
Async XLA Ops:
  0.6 104.2 %copy-start = (bf16[1024,1024]{1,0:T(8,128)(2,1)S(1)}, bf16[1024,1024]{1,0:T(8,128)(2,1)}, u32[]{:S(2)}) copy-start(bf16[1024,1024]{1,0:T(8,128)(2,1)} %param.15) | copy-start | bytes 6291460
  0.6 3.6 %copy-start.1 = (bf16[64,256,128]{2,1,0:T(8,128)(2,1)S(1)}, bf16[64,256,128]{2,1,0:T(8,128)(2,1)}, u32[]{:S(2)}) copy-start(bf16[64,256,128]{2,1,0:T(8,128)(2,1)} %x_ref.1) | copy-start | bytes 12582916
  4.2 4.8 %copy-start.9 = (bf16[128,32]{0,1:T(8,128)(2,1)S(1)}, bf16[128,32]{0,1:T(8,128)(2,1)}, u32[]{:S(2)}) copy-start(bf16[128,32]{0,1:T(8,128)(2,1)} %param.12) | copy-start | bytes 24580
  15.0 7.5 %copy-start.3 = (bf16[64,1024]{1,0:T(8,128)(2,1)S(1)}, bf16[64,1024]{1,0:T(8,128)(2,1)}, u32[]{:S(2)}) copy-start(bf16[64,1024]{1,0:T(8,128)(2,1)} %param.10) | copy-start | bytes 393220
  16.6 20.5 %all-to-all-start.1 = ((bf16[32,64,256]{2,1,0:T(8,128)(2,1)}), bf16[32,64,256]{2,1,0:T(8,128)(2,1)S(1)}, u32[]{:S(2)}, u32[]{:S(2)}) async-start(bf16[32,64,256]{2,1,0:T(8,128)(2,1)} %copy.23), calls=%async_computation.1 | async-start | bytes 2097152 | tf_op jit(solution)/shard_map/all_to_all | solution.py:118
  38.3 40.4 %all-to-all-start = ((bf16[32,2,64,128]{3,2,1,0:T(8,128)(2,1)}), bf16[32,2,64,128]{3,2,1,0:T(8,128)(2,1)}, u32[]{:S(2)}, u32[]{:S(2)}) async-start(bf16[32,2,64,128]{3,2,1,0:T(8,128)(2,1)} %broadcast_in_dim.6), calls=%async_computation | async-start | bytes 2097152 | tf_op jit(solution)/shard_map/all_to_all | solution.py:86
  91.3 1.3 copy-start.2
  92.6 1.0 copy-start.4
  93.7 3.0 %copy-start.6 = (bf16[1024,128]{1,0:T(8,128)(2,1)S(1)}, bf16[1024,128]{1,0:T(8,128)(2,1)}, u32[]{:S(2)}) copy-start(bf16[1024,128]{1,0:T(8,128)(2,1)} %param.14) | copy-start | bytes 786436
  96.5 9.1 %copy-start.7 = (bf16[1024,128]{1,0:T(8,128)(2,1)S(1)}, bf16[1024,128]{1,0:T(8,128)(2,1)}, u32[]{:S(2)}) copy-start(bf16[1024,128]{1,0:T(8,128)(2,1)} %param.16) | copy-start | bytes 786436
  104.8 10.2 %copy-start.8 = (bf16[1024,128]{1,0:T(8,128)(2,1)S(1)}, bf16[1024,128]{1,0:T(8,128)(2,1)}, u32[]{:S(2)}) copy-start(bf16[1024,128]{1,0:T(8,128)(2,1)} %param.16) | copy-start | bytes 786436
  105.4 38.7 %copy-start.5 = (bf16[64,1024]{1,0:T(8,128)(2,1)}, bf16[64,1024]{1,0:T(8,128)(2,1)S(1)}, u32[]{:S(2)}) copy-start(bf16[64,1024]{1,0:T(8,128)(2,1)S(1)} %get-tuple-element.5) | copy-start | bytes 393220
  107.2 20.9 %all-to-all-start.3 = ((bf16[32,2,2048]{2,1,0:T(2,128)(2,1)}), bf16[32,2,2048]{2,1,0:T(2,128)(2,1)S(1)}, u32[]{:S(2)}, u32[]{:S(2)}) async-start(bf16[32,2,2048]{2,1,0:T(2,128)(2,1)} %reshape.73), calls=%async_computation.3 | async-start | bytes 524288 | tf_op jit(solution)/shard_map/all_to_all | solution.py:86

commit v2 on v1

v2 whole, which is shorter than its diff:
```python
import functools
import math

import jax
import jax.numpy as jnp
from jax import lax
from jax.experimental import pallas as pl
from jax.experimental.pallas import tpu as pltpu
from jax.sharding import PartitionSpec as P

EPSILON = 1e-05
F32 = jnp.float32
BF16 = jnp.bfloat16
PAIR_ROWS = 16
PAIR_CHUNK = 4
SCALE = 1.0 / math.sqrt(32)
NT = (((1,), (1,)), ((), ()))
Z_ORDER = (0, 1, 7, 2, 6, 3, 5, 4)


def dot32(a, b):
    return jnp.dot(a, b, preferred_element_type=F32)


def dot_nt(a, b):
    return lax.dot_general(a, b, NT, preferred_element_type=F32)


def norm_rows(values):
    centred = values - jnp.mean(values, axis=-1, keepdims=True)
    variance = jnp.mean(centred * centred, axis=-1, keepdims=True)
    return centred * lax.rsqrt(variance + EPSILON)


def front_kernel(
    seq_hbm, pair_hbm, wbias_hbm, wqkv_hbm, wgate_hbm, wout_hbm, wsp_hbm,
    seq_out_ref, left_ref, right_ref,
    seq_v, pair_v, wbias_v, wqkv_v, wgate_v, wout_v, wsp_v,
    seq32, zbuf, qbuf, gsend, grecv, kv, bias_v, o32, osend, orecv, m_c, l_c, mlsend, mlrecv,
    lrsend, lbuf, rbuf, sosend, sobuf,
    in_sem, pair_sem,
    z_s, z_r, q_s, q_r, g_s, g_r, a_s, kv_r, d_s, o_s, o_r, ml_s, ml_r, l_s, l_r, r_s, r_r, so_s, so_r,
):
    row = lax.axis_index("row")
    col = lax.axis_index("col")
    core = lax.rem(row, 2)
    z = lax.rem(row // 2, 8)
    xh = row // 16
    partner = row + 1 - 2 * core
    own_plane = xh == col // 4
    own_right = row // 4 == col

    loads = [
        pltpu.make_async_copy(src, dst, in_sem.at[n])
        for n, (src, dst) in enumerate(
            ((seq_hbm, seq_v), (wqkv_hbm, wqkv_v), (wgate_hbm, wgate_v), (wbias_hbm, wbias_v),
             (wout_hbm, wout_v), (wsp_hbm, wsp_v))
        )
    ]
    for n in range(4):
        loads[n].start()

    barrier = pltpu.get_barrier_semaphore()

    def greet(r, c):
        pl.semaphore_signal(barrier, inc=1, device_id=(r, c), device_id_type=pl.DeviceIdType.MESH)

    def z_row(k):
        return xh * 16 + lax.rem(z + k, 8) * 2 + core

    for d in range(1, 8):
        greet(z_row(d), col)
        greet(row, lax.rem(col + d, 8))
    greet(partner, col)
    plane_row = (col // 4) * 16 + z * 2 + core
    for c in range(8):
        @pl.when(jnp.logical_not(jnp.logical_and(own_plane, col == c)))
        def _():
            greet(plane_row, c)

    @pl.loop(0, 32)
    def _(n):
        r, c = 4 * col + n // 8, lax.rem(n, 8)

        @pl.when(jnp.logical_not(jnp.logical_and(own_right, jnp.logical_and(row == r, col == c))))
        def _():
            greet(r, c)

    def pair_load(n):
        return pltpu.make_async_copy(pair_hbm.at[pl.ds(n * 8, 8)], pair_v.at[pl.ds(n * 8, 8)], pair_sem.at[n])

    for n in range(8):
        pair_load(n).start()
    for n in (4, 5):
        loads[n].start()

    lane = lax.broadcasted_iota(jnp.int32, (1, 128), 1)
    loads[0].wait()
    x = seq_v[...].astype(F32)
    seq32[...] = x
    normed = norm_rows(x).astype(BF16)
    loads[1].wait()
    zbuf[0, 0:64] = dot32(normed, wqkv_v[1]).astype(BF16)
    zbuf[0, 64:128] = dot32(normed, wqkv_v[2]).astype(BF16)
    qbuf[0] = dot32(normed, wqkv_v[0]).astype(BF16)

    pl.semaphore_wait(
        barrier, 15 + 8 - own_plane.astype(jnp.int32) + 32 - own_right.astype(jnp.int32)
    )

    def remote(src, dst, ss, rs, r, c):
        return pltpu.make_async_remote_copy(
            src_ref=src, dst_ref=dst, send_sem=ss, recv_sem=rs, device_id=(r, c),
            device_id_type=pl.DeviceIdType.MESH,
        )

    def z_copy(d):
        return remote(zbuf.at[0], zbuf.at[d], z_s.at[d], z_r.at[d], z_row(d), col)

    def col_copy(src, dst, ss, rs, d):
        return remote(src, dst, ss.at[d], rs.at[d], row, lax.rem(col + d, 8))

    def q_copy(d):
        return col_copy(qbuf.at[0], qbuf.at[d], q_s, q_r, d)

    def g_copy(d):
        return col_copy(gsend.at[lax.rem(col + d, 8)], grecv.at[d], g_s, g_r, d)

    for d in (4, 3, 5, 2, 6, 1, 7):
        z_copy(d).start()

    loads[2].wait()
    gate = jax.nn.sigmoid(dot32(normed, wgate_v[...]))
    gsend[...] = gate.reshape(8, 8, 128)

    loads[3].wait()
    wb = wbias_v[...].astype(F32)
    wb_t = jnp.concatenate([wb, jnp.zeros((128, 96), F32)], axis=1).T[0:32].astype(BF16)
    ia = lax.broadcasted_iota(jnp.int32, (128, 128), 0)
    ib = lax.broadcasted_iota(jnp.int32, (128, 128), 1)
    centre = (jnp.where(ia == ib, 1.0, 0.0) - 1.0 / 128).astype(BF16)

    def bias_row(i):
        ct = dot_nt(centre, pair_v[i])
        variance = jnp.mean(ct * ct, axis=0, keepdims=True)
        n = (ct * lax.rsqrt(variance + EPSILON)).astype(BF16)
        b = dot32(wb_t, n).astype(BF16).astype(F32)
        bias_v[0, pl.ds(i, 32, stride=64), :] = b[:, 0:128]
        bias_v[1, pl.ds(i, 32, stride=64), :] = b[:, 128:256]

    def plane_copy(d, k):
        source = lax.rem(z + 8 - d, 8)
        return remote(
            zbuf.at[d], kv.at[lax.rem(source, 2) * 2 + core, col], a_s.at[d, k],
            kv_r.at[lax.rem(source, 2) * 2 + core, col], k * 16 + z * 2 + core, xh * 4 + source // 2,
        )

    def to_self(d, k):
        source = lax.rem(z + 8 - d, 8)
        return jnp.logical_and(xh == k, col == xh * 4 + source // 2)

    for step, d in enumerate(Z_ORDER):
        if d:
            z_copy(d).wait_recv()
        for k in range(2):
            here = to_self(d, k)

            @pl.when(here)
            def _():
                kv[lax.rem(z + 8 - d, 2) * 2 + core, col] = zbuf[d]

            @pl.when(jnp.logical_not(here))
            def _():
                plane_copy(d, k).start()

        if step == 0:
            for e in (4, 3, 5, 2, 6, 1, 7):
                q_copy(e).start()
        if step == 1:
            for e in (4, 3, 5, 2, 6, 1, 7):
                g_copy(e).start()
        pair_load(step).wait()

        @pl.loop(0, 8)
        def _(n):
            bias_row(step * 8 + n)

    def kv_wait(q, c):
        return remote(kv.at[q, c], kv.at[q, c], d_s.at[0, 0], kv_r.at[q, c], partner, col)

    def core_copy(h, c):
        q = h * 2 + core
        return remote(kv.at[q, c], kv.at[q, c], d_s.at[h, c], kv_r.at[q, c], partner, col)

    for h in range(2):
        @pl.loop(0, 8)
        def _(c):
            @pl.when(jnp.logical_not(jnp.logical_and(own_plane, col == c)))
            def _():
                kv_wait(h * 2 + core, c).wait_recv()

            core_copy(h, c).start()

    for d in range(1, 8):
        q_copy(d).wait_recv()
    for h in range(2):
        @pl.loop(0, 8)
        def _(c):
            kv_wait(h * 2 + 1 - core, c).wait_recv()

    m_c[...] = jnp.zeros_like(m_c)
    l_c[...] = jnp.ones_like(l_c)
    head_of = lane // 32

    @pl.loop(0, 8)
    def _(d):
        g = lax.rem(col + 8 - d, 8)
        q = qbuf[d].astype(F32)
        q4 = jnp.concatenate([jnp.where(head_of == t, q, 0.0) for t in range(4)], axis=0).astype(BF16)
        blocks = [kv[b, g] for b in range(4)]
        keys = jnp.concatenate([b[0:64] for b in blocks], axis=0)
        values = jnp.concatenate([b[64:128] for b in blocks], axis=0)
        at = pl.ds(pl.multiple_of(g * 256, 256), 256)
        bias = jnp.concatenate([bias_v[0, at], bias_v[1, at]], axis=1)
        scores = dot_nt(q4, keys) * SCALE + bias
        peak = jnp.max(scores, axis=1, keepdims=True)
        weights = jnp.exp(scores - peak)
        total = jnp.sum(weights, axis=1, keepdims=True)
        o4 = dot32(weights.astype(BF16), values)
        out = jnp.zeros((64, 128), F32)
        m, l = m_c[...], l_c[...]
        for t in range(4):
            part = slice(t * 64, t * 64 + 64)
            out = jnp.where(head_of == t, o4[part], out)
            m = jnp.where(lane == g * 4 + t, peak[part], m)
            l = jnp.where(lane == g * 4 + t, total[part], l)
        m_c[...] = m
        l_c[...] = l
        o32[:, pl.ds(pl.multiple_of(g * 8, 8), 8), :] = out.reshape(8, 8, 128)

    osend[...] = o32[...].astype(BF16)
    mlsend[:, 0:8] = m_c[...].reshape(8, 8, 128)
    mlsend[:, 8:16] = l_c[...].reshape(8, 8, 128)

    def o_copy(d):
        return col_copy(osend.at[lax.rem(col + d, 8)], orecv.at[d], o_s, o_r, d)

    def ml_copy(d):
        return col_copy(mlsend.at[lax.rem(col + d, 8)], mlrecv.at[d], ml_s, ml_r, d)

    for d in (4, 3, 5, 2, 6, 1, 7):
        ml_copy(d).start()
        o_copy(d).start()
    orecv[0] = osend[col]
    mlrecv[0] = mlsend[col]
    grecv[0] = gsend[col]
    ea = lax.broadcasted_iota(jnp.int32, (128, 1024), 0)
    eb = lax.broadcasted_iota(jnp.int32, (128, 1024), 1)
    expand = jnp.where(ea == eb // 32, 1.0, 0.0).astype(BF16)
    for d in range(1, 8):
        g_copy(d).wait_recv()
        ml_copy(d).wait_recv()
        o_copy(d).wait_recv()

    peaks = [mlrecv[p, 0:8] for p in range(8)]
    top = functools.reduce(jnp.maximum, peaks)
    shares = [jnp.exp(v - top) for v in peaks]
    whole = functools.reduce(jnp.add, [s * mlrecv[p, 8:16] for p, s in enumerate(shares)])
    share = jnp.concatenate([s / whole for s in shares], axis=0)
    high = share.astype(BF16)
    low = (share - high.astype(F32)).astype(BF16)
    wide = dot32(high, expand) + dot32(low, expand)
    parts = []
    for g in range(8):
        tile = jnp.zeros((8, 128), F32)
        for p in range(8):
            tile = tile + wide[p * 8 : p * 8 + 8, g * 128 : g * 128 + 128] * orecv[p].astype(F32)[g * 8 : g * 8 + 8]
        parts.append(tile * grecv[lax.rem(col + 8 - g, 8)])
    attended = jnp.concatenate(parts, axis=1).astype(BF16)
    loads[4].wait()
    update = dot32(attended, wout_v[...])
    new_seq = (seq32[pl.ds(pl.multiple_of(col * 8, 8), 8), :] + update).astype(BF16).astype(F32)
    new_normed = norm_rows(new_seq).astype(BF16)
    loads[5].wait()
    sides = dot32(new_normed, wsp_v[...]).astype(BF16).astype(F32)
    lrsend[...] = sides

    def r_copy(n):
        return remote(lrsend, rbuf.at[lax.rem(row, 4), col], r_s.at[n], r_r.at[lax.rem(row, 4), col], n, row // 4)

    def l_copy(d):
        return remote(lrsend, lbuf.at[col], l_s.at[d], l_r.at[col], row, lax.rem(col + d, 8))

    def so_copy(d):
        return remote(sosend, sobuf.at[col], so_s.at[d], so_r.at[col], row, lax.rem(col + d, 8))

    def right_here(n):
        return jnp.logical_and(own_right, row == n)

    @pl.loop(0, 32)
    def _(n):
        @pl.when(jnp.logical_not(right_here(n)))
        def _():
            r_copy(n).start()

    for d in (4, 3, 5, 2, 6, 1, 7):
        l_copy(d).start()
    sosend[...] = jnp.concatenate([new_seq[:, g * 128 : g * 128 + 128] for g in range(8)], axis=0).astype(BF16)
    for d in (4, 3, 5, 2, 6, 1, 7):
        so_copy(d).start()
    lbuf[col] = sides
    sobuf[col] = sosend[...]

    @pl.when(own_right)
    def _():
        rbuf[lax.rem(row, 4), col] = sides

    for d in range(1, 8):
        z_copy(d).wait_send()
        q_copy(d).wait_send()
        g_copy(d).wait_send()
        ml_copy(d).wait_send()
        o_copy(d).wait_send()
    for d in range(8):
        for k in range(2):
            @pl.when(jnp.logical_not(to_self(d, k)))
            def _():
                plane_copy(d, k).wait_send()
    for h in range(2):
        @pl.loop(0, 8)
        def _(c):
            core_copy(h, c).wait_send()

    def col_wait(buf, ss, rs, d):
        source = lax.rem(col + 8 - d, 8)
        return remote(buf.at[source], buf.at[source], ss.at[d], rs.at[source], row, source)

    for d in range(1, 8):
        col_wait(lbuf, l_s, l_r, d).wait_recv()
        col_wait(sobuf, so_s, so_r, d).wait_recv()
    left_ref[...] = lbuf[...].reshape(64, 128)
    for c in range(8):
        block = sobuf[c].astype(F32)
        o32[c] = block
    seq_out_ref[...] = jnp.concatenate(
        [o32[:, g * 8 : g * 8 + 8, :].reshape(64, 128) for g in range(8)], axis=1
    ).astype(BF16)
    for q in range(4):
        @pl.loop(0, 8)
        def _(c):
            @pl.when(jnp.logical_not(jnp.logical_and(own_right, jnp.logical_and(lax.rem(row, 4) == q, col == c))))
            def _():
                remote(rbuf.at[q, c], rbuf.at[q, c], r_s.at[0], r_r.at[q, c], partner, col).wait_recv()

    right_ref[...] = rbuf[...].reshape(256, 128)
    for d in range(1, 8):
        l_copy(d).wait_send()
        so_copy(d).wait_send()

    @pl.loop(0, 32)
    def _(n):
        @pl.when(jnp.logical_not(right_here(n)))
        def _():
            r_copy(n).wait_send()


def front(seq_state, pair_state, w_bias, w_qkv, w_gate, w_out, w_seq_pair):
    any_spec = pl.BlockSpec(memory_space=pl.ANY)
    vmem_spec = pl.BlockSpec(memory_space=pltpu.VMEM)
    dma = pltpu.SemaphoreType.DMA
    return pl.pallas_call(
        front_kernel,
        out_shape=(
            jax.ShapeDtypeStruct((64, 1024), BF16),
            jax.ShapeDtypeStruct((64, 128), F32),
            jax.ShapeDtypeStruct((256, 128), F32),
        ),
        in_specs=[any_spec] * 7,
        out_specs=(vmem_spec,) * 3,
        scratch_shapes=[
            pltpu.VMEM((64, 1024), BF16),
            pltpu.VMEM((64, 256, 128), BF16),
            pltpu.VMEM((128, 32), BF16),
            pltpu.VMEM((3, 1024, 128), BF16),
            pltpu.VMEM((1024, 128), BF16),
            pltpu.VMEM((1024, 1024), BF16),
            pltpu.VMEM((1024, 128), BF16),
            pltpu.VMEM((64, 1024), F32),
            pltpu.VMEM((8, 128, 128), BF16),
            pltpu.VMEM((8, 64, 128), BF16),
            pltpu.VMEM((8, 8, 128), F32),
            pltpu.VMEM((8, 8, 128), F32),
            pltpu.VMEM((4, 8, 128, 128), BF16),
            pltpu.VMEM((2, 2048, 128), F32),
            pltpu.VMEM((8, 64, 128), F32),
            pltpu.VMEM((8, 64, 128), BF16),
            pltpu.VMEM((8, 64, 128), BF16),
            pltpu.VMEM((64, 128), F32),
            pltpu.VMEM((64, 128), F32),
            pltpu.VMEM((8, 16, 128), F32),
            pltpu.VMEM((8, 16, 128), F32),
            pltpu.VMEM((8, 128), F32),
            pltpu.VMEM((8, 8, 128), F32),
            pltpu.VMEM((4, 8, 8, 128), F32),
            pltpu.VMEM((64, 128), BF16),
            pltpu.VMEM((8, 64, 128), BF16),
            dma((6,)), dma((8,)),
            dma((8,)), dma((8,)), dma((8,)), dma((8,)), dma((8,)), dma((8,)),
            dma((8, 2)), dma((4, 8)), dma((2, 8)),
            dma((8,)), dma((8,)), dma((8,)), dma((8,)), dma((8,)), dma((8,)),
            dma((32,)), dma((4, 8)), dma((8,)), dma((8,)),
        ],
        compiler_params=pltpu.CompilerParams(
            collective_id=0, has_side_effects=True, vmem_limit_bytes=48 * 1024 * 1024
        ),
        cost_estimate=pl.CostEstimate(flops=3_000_000_000, bytes_accessed=8_000_000, transcendentals=600_000),
    )(seq_state, pair_state, w_bias, w_qkv, w_gate, w_out, w_seq_pair)


def pair_kernel(x_ref, left_ref, right_ref, wp_ref, wu_ref, wd_ref, o_ref, mix_ref, right2_ref):
    @pl.when(pl.program_id(0) == 0)
    def _():
        w = wp_ref[...].astype(F32)
        centred = w - jnp.mean(w, axis=1, keepdims=True)
        a = lax.broadcasted_iota(jnp.int32, (128, 128), 0)
        b = lax.broadcasted_iota(jnp.int32, (128, 128), 1)
        eye = jnp.where(a == b, 1.0, 0.0)
        mix_ref[0:128, 0:128] = (eye - 1.0 / 128).astype(BF16)
        mix_ref[0:128, 128:256] = eye.astype(BF16)
        mix_ref[128:256, 0:128] = centred.astype(BF16)
        mix_ref[128:256, 128:256] = wp_ref[...]
        r = right_ref[:, 64:128]
        right2_ref[...] = jnp.concatenate([r, r], axis=1)

    lane = lax.broadcasted_iota(jnp.int32, (1, 128), 1)
    for start in range(0, PAIR_ROWS, PAIR_CHUNK):
        features, rows = [], []
        for i in range(start, start + PAIR_CHUNK):
            left = left_ref[pl.ds(i, 1), 0:64]
            left2 = jnp.concatenate([left, left], axis=1)
            scale = jnp.where(lane < 64, left2, -1.0)
            shift = jnp.where(lane < 64, 0.0, left2)
            features.append((right2_ref[...] * scale + shift).astype(BF16))
            rows.append(x_ref[i])
        mixed = dot32(
            jnp.concatenate([jnp.concatenate(rows, axis=0), jnp.concatenate(features, axis=0)], axis=1),
            mix_ref[...],
        )
        centred, updated = mixed[:, :128], mixed[:, 128:]
        variance = jnp.mean(centred * centred, axis=1, keepdims=True)
        normed = (centred * lax.rsqrt(variance + EPSILON)).astype(BF16)
        hidden = jnp.maximum(dot32(normed, wu_ref[...]), 0.0).astype(BF16)
        result = (updated + dot32(hidden, wd_ref[...])).astype(BF16)
        for i in range(PAIR_CHUNK):
            o_ref[start + i] = result[i * 256 : (i + 1) * 256]


def pair_transition(x, left, right, wp, wu, wd):
    rows = x.shape[0]

    def whole(array):
        return pl.BlockSpec(array.shape, lambda i: (0,) * array.ndim)

    return pl.pallas_call(
        pair_kernel,
        grid=(rows // PAIR_ROWS,),
        out_shape=jax.ShapeDtypeStruct(x.shape, BF16),
        in_specs=[
            pl.BlockSpec((PAIR_ROWS, 256, 128), lambda i: (i, 0, 0)),
            pl.BlockSpec((PAIR_ROWS, 128), lambda i: (i, 0)),
            whole(right),
            whole(wp),
            whole(wu),
            whole(wd),
        ],
        out_specs=pl.BlockSpec((PAIR_ROWS, 256, 128), lambda i: (i, 0, 0)),
        scratch_shapes=[pltpu.VMEM((256, 256), BF16), pltpu.VMEM((256, 128), F32)],
        compiler_params=pltpu.CompilerParams(dimension_semantics=("arbitrary",)),
    )(x, left, right, wp, wu, wd)


def body(seq_state, pair_state, w_bias, w_qkv, w_gate, w_out, w_seq_pair, w_pair_out, w_up, w_down):
    seq_out, left, right = front(seq_state, pair_state, w_bias, w_qkv, w_gate, w_out, w_seq_pair)
    return (seq_out, pair_transition(pair_state, left, right, w_pair_out, w_up, w_down))


def solution(mesh):
    return jax.shard_map(
        body,
        mesh=mesh,
        in_specs=(
            P("row", None),
            P("row", "col", None),
            P(),
            P(None, None, "col"),
            P(None, "col"),
            P(),
            P(),
            P(),
            P(),
            P(),
        ),
        out_specs=(P("row", None), P("row", "col", None)),
        check_vma=False,
    )
```

time: 145 us -> 87 us (0.60)
  Pallas kernels: 15 us -> 77.8 us
  waiting for transfers between devices: 45.4 us -> 0 us
  starting transfers between devices: 26.7 us -> 0 us
  matrix products: 16.6 us -> 0 us
  local copies, waits for them, and re-layouts: 22.2 us -> 8.24 us
  other arithmetic: 9.29 us -> 0 us
  blocking collectives: 7.94 us -> 0 us
    pallas_call x0 -> x1, Pallas kernels: none -> 62.5 us  [front(): pl.pallas_call(front_kernel, out_shape=(jax.ShapeDtypeStruct((64, 1024),...]
    all_to_all x3 -> x0, waiting for transfers between devices: 45.4 us -> none  [the longest x2 33.6 us: sent_to_all(): lax.all_to_all(jnp.broadcast_to(x[None], (peers, *x.shape)), axis, 0, 0,...]
    all_to_all x3 -> x0, starting transfers between devices: 26.7 us -> none  [the longest x2 20.7 us: sent_to_all(): lax.all_to_all(jnp.broadcast_to(x[None], (peers, *x.shape)), axis, 0, 0,...]
    dot_general x10 -> x0, matrix products: 16.6 us -> none  [the longest x1 5.97 us: body(): jnp.einsum('rcp,ph->hrc', pair_normed, w_bias, preferred_element_type=jnp...]
    reduce_sum x5 -> x0, other arithmetic: 8.77 us -> none  [the longest x3 5.13 us: layer_norm(): variance = jnp.mean(centred * centred, axis=-1, keepdims=True)]
    all_to_all x1 -> x0, blocking collectives: 7.94 us -> none  [sent_to_all(): lax.all_to_all(jnp.broadcast_to(x[None], (peers, *x.shape)), axis, 0, 0,...]
    slice x3 -> x0, local copies, waits for them, and re-layouts: 7.15 us -> none  [the longest x2 4.69 us: body(): key_heads = key_value[0].reshape(length, local_heads, head_size)]
    convert_element_type x4 -> x0, local copies, waits for them, and re-layouts: 6.35 us -> none  [the longest x2 4.68 us: body(): bias_rows.astype(jnp.float32)]
  transfers between devices with their start and end apart: 3 -> 0, of which waited for: 3 -> 0; matrix products, arithmetic and copies ran while one was open for 7% -> 0% of each run, Pallas kernels for 0% -> 0%
where the time goes in v2:
time: 87 us; the launch traced here: 86.7 us
  Pallas kernels  77.8 us (89%)
  local copies, waits for them, and re-layouts  8.24 us (9%)
    pallas_call x1, Pallas kernels, front(): pl.pallas_call(front_kernel, out_shape=(jax.ShapeDtypeStruct((64, 1024),...  62.5 us
    pallas_call x1, Pallas kernels, pair_transition(): pl.pallas_call(pair_kernel, grid=(rows // PAIR_ROWS,), out_shape=jax.Shap...  15.2 us
    unnamed x16, local copies, waits for them, and re-layouts  8.24 us

profile of v2, /device:TPU:1, one launch (start us, length us, event | category | flops | bytes accessed | tf_op | source)
XLA Modules:
  0.0 86.7 jit_solution(2066924165411559931)
XLA Ops:
  0.6 0.8 copy.12.wbias_hbm
  1.4 0.0 copy-start.2
  1.4 1.6 %copy-done.2 = bf16[1024,1024]{1,0:T(8,128)(2,1)S(1)} copy-done((bf16[1024,1024]{1,0:T(8,128)(2,1)S(1)}, bf16[1024,1024]{1,0:T(8,128)(2,1)}, u32[]{:S(2)}) %copy-start.2) | copy-done | bytes 2097176
  3.0 0.0 copy-start.3
  3.0 1.1 %copy-done.3 = bf16[3,1024,128]{2,1,0:T(8,128)(2,1)S(1)} copy-done((bf16[3,1024,128]{2,1,0:T(8,128)(2,1)S(1)}, bf16[3,1024,128]{2,1,0:T(8,128)(2,1)}, u32[]{:S(2)}) %copy-start.3) | copy-done | bytes 786456
  4.2 0.0 copy-start.4
  4.2 0.9 %copy-done.4 = bf16[1024,128]{1,0:T(8,128)(2,1)S(1)} copy-done((bf16[1024,128]{1,0:T(8,128)(2,1)S(1)}, bf16[1024,128]{1,0:T(8,128)(2,1)}, u32[]{:S(2)}) %copy-start.4) | copy-done | bytes 262168
  5.1 0.0 copy-start.5
  5.1 0.9 %copy-done.5 = bf16[1024,128]{1,0:T(8,128)(2,1)S(1)} copy-done((bf16[1024,128]{1,0:T(8,128)(2,1)S(1)}, bf16[1024,128]{1,0:T(8,128)(2,1)}, u32[]{:S(2)}) %copy-start.5) | copy-done | bytes 262168
  6.1 0.0 copy-start.6
  6.1 0.9 %copy-done.6 = bf16[64,1024]{1,0:T(8,128)(2,1)S(1)} copy-done((bf16[64,1024]{1,0:T(8,128)(2,1)S(1)}, bf16[64,1024]{1,0:T(8,128)(2,1)}, u32[]{:S(2)}) %copy-start.6) | copy-done | bytes 131096
  7.0 62.5 %shard_map.113 = (bf16[64,1024]{1,0:T(8,128)(2,1)S(1)}, f32[64,128]{1,0:T(8,128)S(1)}, f32[256,128]{1,0:T(8,128)S(1)}) custom-call(bf16[64,1024]{1,0:T(8,128)(2,1)S(1)} %copy-done.6, bf16[64,256,128]{2,1,0:T(8,128)(2,1)} %x_ref.1, bf16[128,32]{1,0:T(8,128)(2,1)S(1)} %copy.12.wbias_hbm, bf16[3,1024,128]{2,1,0:T(8,128)(2,1)S(1)} %copy-done.3, ...), custom_call_target="tpu_custom_call" | custom-call | flops 3000000000 | bytes 8000000 | tf_op jit(solution)/shard_map/pallas_call | solution.py:371
  69.5 0.0 copy-start
  69.5 0.6 copy-done
  70.2 0.0 copy-start.1
  70.2 0.6 copy-done.1
  70.8 15.2 %shard_map.114 = bf16[64,256,128]{2,1,0:T(8,128)(2,1)} custom-call(bf16[64,256,128]{2,1,0:T(8,128)(2,1)} %x_ref.1, f32[64,128]{1,0:T(8,128)} %copy-done.1, f32[256,128]{1,0:T(8,128)} %copy-done, bf16[128,128]{1,0:T(8,128)(2,1)} %wp_ref.1, bf16[128,512]{1,0:T(8,128)(2,1)} %wu_ref.1, bf16[512,128]{1,0:T(8,128)(2,1)} %wd_ref.1), custom_call_target="tpu_custom_call" | custom-call | tf_op jit(solution)/shard_map/pallas_call | solution.py:464
  86.0 0.7 copy.14
Async XLA Ops:
  1.4 1.6 %copy-start.2 = (bf16[1024,1024]{1,0:T(8,128)(2,1)S(1)}, bf16[1024,1024]{1,0:T(8,128)(2,1)}, u32[]{:S(2)}) copy-start(bf16[1024,1024]{1,0:T(8,128)(2,1)} %wout_hbm.1) | copy-start | bytes 6291460
  3.0 1.1 %copy-start.3 = (bf16[3,1024,128]{2,1,0:T(8,128)(2,1)S(1)}, bf16[3,1024,128]{2,1,0:T(8,128)(2,1)}, u32[]{:S(2)}) copy-start(bf16[3,1024,128]{2,1,0:T(8,128)(2,1)} %wqkv_hbm.1) | copy-start | bytes 2359300
  4.2 0.9 %copy-start.4 = (bf16[1024,128]{1,0:T(8,128)(2,1)S(1)}, bf16[1024,128]{1,0:T(8,128)(2,1)}, u32[]{:S(2)}) copy-start(bf16[1024,128]{1,0:T(8,128)(2,1)} %wgate_hbm.1) | copy-start | bytes 786436
  5.1 0.9 %copy-start.5 = (bf16[1024,128]{1,0:T(8,128)(2,1)S(1)}, bf16[1024,128]{1,0:T(8,128)(2,1)}, u32[]{:S(2)}) copy-start(bf16[1024,128]{1,0:T(8,128)(2,1)} %wsp_hbm.1) | copy-start | bytes 786436
  6.1 0.9 %copy-start.6 = (bf16[64,1024]{1,0:T(8,128)(2,1)S(1)}, bf16[64,1024]{1,0:T(8,128)(2,1)}, u32[]{:S(2)}) copy-start(bf16[64,1024]{1,0:T(8,128)(2,1)} %seq_hbm.1) | copy-start | bytes 393220
  69.5 0.7 copy-start
  70.2 0.6 copy-start.1

commit v3 on v2

--- a/solution.py
+++ b/solution.py
@@ -15,7 +15,7 @@
 PAIR_CHUNK = 4
 SCALE = 1.0 / math.sqrt(32)
 NT = (((1,), (1,)), ((), ()))
-Z_ORDER = (0, 1, 7, 2, 6, 3, 5, 4)
+NEAR_FIRST = (1, 7, 2, 6, 3, 5, 4)
 
 
 def dot32(a, b):
@@ -126,7 +126,7 @@
     def g_copy(d):
         return col_copy(gsend.at[lax.rem(col + d, 8)], grecv.at[d], g_s, g_r, d)
 
-    for d in (4, 3, 5, 2, 6, 1, 7):
+    for d in NEAR_FIRST:
         z_copy(d).start()
 
     loads[2].wait()
@@ -134,19 +134,20 @@
     gsend[...] = gate.reshape(8, 8, 128)
 
     loads[3].wait()
-    wb = wbias_v[...].astype(F32)
-    wb_t = jnp.concatenate([wb, jnp.zeros((128, 96), F32)], axis=1).T[0:32].astype(BF16)
+    wb_t = wbias_v[...]
     ia = lax.broadcasted_iota(jnp.int32, (128, 128), 0)
     ib = lax.broadcasted_iota(jnp.int32, (128, 128), 1)
     centre = (jnp.where(ia == ib, 1.0, 0.0) - 1.0 / 128).astype(BF16)
 
-    def bias_row(i):
-        ct = dot_nt(centre, pair_v[i])
-        variance = jnp.mean(ct * ct, axis=0, keepdims=True)
-        n = (ct * lax.rsqrt(variance + EPSILON)).astype(BF16)
-        b = dot32(wb_t, n).astype(BF16).astype(F32)
-        bias_v[0, pl.ds(i, 32, stride=64), :] = b[:, 0:128]
-        bias_v[1, pl.ds(i, 32, stride=64), :] = b[:, 128:256]
+    def bias_rows(n):
+        pair_load(n).wait()
+        c = dot32(pair_v[n * 8 : n * 8 + 8].reshape(2048, 128), centre)
+        variance = jnp.mean(c * c, axis=1, keepdims=True)
+        b = dot_nt(wb_t, (c * lax.rsqrt(variance + EPSILON)).astype(BF16)).astype(BF16).astype(F32)
+        for i in range(8):
+            for half in range(2):
+                at = i * 256 + half * 128
+                bias_v[half, pl.ds(n * 8 + i, 32, stride=64), :] = b[:, at : at + 128]
 
     def plane_copy(d, k):
         source = lax.rem(z + 8 - d, 8)
@@ -159,7 +160,7 @@
         source = lax.rem(z + 8 - d, 8)
         return jnp.logical_and(xh == k, col == xh * 4 + source // 2)
 
-    for step, d in enumerate(Z_ORDER):
+    def forward(d):
         if d:
             z_copy(d).wait_recv()
         for k in range(2):
@@ -173,17 +174,18 @@
             def _():
                 plane_copy(d, k).start()
 
-        if step == 0:
-            for e in (4, 3, 5, 2, 6, 1, 7):
-                q_copy(e).start()
-        if step == 1:
-            for e in (4, 3, 5, 2, 6, 1, 7):
-                g_copy(e).start()
-        pair_load(step).wait()
-
-        @pl.loop(0, 8)
-        def _(n):
-            bias_row(step * 8 + n)
+    forward(0)
+    for e in NEAR_FIRST:
+        q_copy(e).start()
+    for e in NEAR_FIRST:
+        g_copy(e).start()
+    bias_rows(0)
+    for n, pair in enumerate(((1, 7), (2, 6), (3, 5), (4,))):
+        for d in pair:
+            forward(d)
+        bias_rows(n + 1)
+    for n in range(5, 8):
+        bias_rows(n)
 
     def kv_wait(q, c):
         return remote(kv.at[q, c], kv.at[q, c], d_s.at[0, 0], kv_r.at[q, c], partner, col)
@@ -212,7 +214,7 @@
     l_c[...] = jnp.ones_like(l_c)
     head_of = lane // 32
 
-    @pl.loop(0, 8)
+    @pl.loop(0, 8, unroll=4)
     def _(d):
         g = lax.rem(col + 8 - d, 8)
         q = qbuf[d].astype(F32)
@@ -380,7 +382,7 @@
         scratch_shapes=[
             pltpu.VMEM((64, 1024), BF16),
             pltpu.VMEM((64, 256, 128), BF16),
-            pltpu.VMEM((128, 32), BF16),
+            pltpu.VMEM((32, 128), BF16),
             pltpu.VMEM((3, 1024, 128), BF16),
             pltpu.VMEM((1024, 128), BF16),
             pltpu.VMEM((1024, 1024), BF16),
@@ -411,7 +413,7 @@
             dma((32,)), dma((4, 8)), dma((8,)), dma((8,)),
         ],
         compiler_params=pltpu.CompilerParams(
-            collective_id=0, has_side_effects=True, vmem_limit_bytes=48 * 1024 * 1024
+            collective_id=0, has_side_effects=True, vmem_limit_bytes=67_043_328
         ),
         cost_estimate=pl.CostEstimate(flops=3_000_000_000, bytes_accessed=8_000_000, transcendentals=600_000),
     )(seq_state, pair_state, w_bias, w_qkv, w_gate, w_out, w_seq_pair)
@@ -480,7 +482,7 @@
 
 
 def body(seq_state, pair_state, w_bias, w_qkv, w_gate, w_out, w_seq_pair, w_pair_out, w_up, w_down):
-    seq_out, left, right = front(seq_state, pair_state, w_bias, w_qkv, w_gate, w_out, w_seq_pair)
+    seq_out, left, right = front(seq_state, pair_state, w_bias.T, w_qkv, w_gate, w_out, w_seq_pair)
     return (seq_out, pair_transition(pair_state, left, right, w_pair_out, w_up, w_down))
 
 

time: 87 us -> 61.9 us (0.71)
  Pallas kernels: 77.8 us -> 60.1 us
  local copies, waits for them, and re-layouts: 8.24 us -> 0.66 us
    pallas_call x1, Pallas kernels: 62.5 us -> 44.8 us  [front(): pl.pallas_call(front_kernel, out_shape=(jax.ShapeDtypeStruct((64, 1024),...]
    unnamed x16 -> x3, local copies, waits for them, and re-layouts: 8.24 us -> 0.66 us
where the time goes in v3:
time: 61.9 us; the launch traced here: 61.4 us
  Pallas kernels  60.1 us (97%)
  local copies, waits for them, and re-layouts  0.66 us (1%)
  between operations  0.65 us (1%)
    pallas_call x1, Pallas kernels, front(): pl.pallas_call(front_kernel, out_shape=(jax.ShapeDtypeStruct((64, 1024),...  44.8 us
    pallas_call x1, Pallas kernels, pair_transition(): pl.pallas_call(pair_kernel, grid=(rows // PAIR_ROWS,), out_shape=jax.Shap...  15.3 us

profile of v3, /device:TPU:1, one launch (start us, length us, event | category | flops | bytes accessed | tf_op | source)
XLA Modules:
  0.0 61.4 jit_solution(9554015228856947791)
XLA Ops:
  0.6 44.8 %shard_map.113 = (bf16[64,1024]{1,0:T(8,128)(2,1)}, f32[64,128]{1,0:T(8,128)}, f32[256,128]{1,0:T(8,128)}) custom-call(bf16[64,1024]{1,0:T(8,128)(2,1)} %seq_hbm.1, bf16[64,256,128]{2,1,0:T(8,128)(2,1)} %x_ref.1, bf16[32,128]{1,0:T(8,128)(2,1)} %bitcast.1, bf16[3,1024,128]{2,1,0:T(8,128)(2,1)} %wqkv_hbm.1, bf16[1024,128]{1,0:T(8,128)(2,1)} %wgate_hbm.1, ...), custom_call_target="tpu_custom_call" | custom-call | flops 3000000000 | bytes 8000000 | tf_op jit(solution)/shard_map/pallas_call | solution.py:373
  45.4 0.0 copy-start
  45.4 15.3 %shard_map.114 = bf16[64,256,128]{2,1,0:T(8,128)(2,1)} custom-call(bf16[64,256,128]{2,1,0:T(8,128)(2,1)} %x_ref.1, f32[64,128]{1,0:T(8,128)} %get-tuple-element.6.left_ref, f32[256,128]{1,0:T(8,128)} %get-tuple-element.7.right_ref, bf16[128,128]{1,0:T(8,128)(2,1)} %wp_ref.1, bf16[128,512]{1,0:T(8,128)(2,1)} %wu_ref.1, bf16[512,128]{1,0:T(8,128)(2,1)} %wd_ref.1), custom_call_target="tpu_custom_call" | custom-call | tf_op jit(solution)/shard_map/pallas_call | solution.py:466
  60.7 0.0 copy-done
  60.7 0.7 %copy.13 = bf16[64,1024]{1,0:T(8,128)(2,1)} copy(bf16[64,1024]{1,0:T(8,128)(2,1)S(1)} %copy-done) | data formatting | bytes 262144
Async XLA Ops:
  45.4 15.3 %copy-start = (bf16[64,1024]{1,0:T(8,128)(2,1)S(1)}, bf16[64,1024]{1,0:T(8,128)(2,1)}, u32[]{:S(2)}) copy-start(bf16[64,1024]{1,0:T(8,128)(2,1)} %get-tuple-element.10) | copy-start | bytes 393220

commit v4 on v3

--- a/solution.py
+++ b/solution.py
@@ -16,6 +16,7 @@
 SCALE = 1.0 / math.sqrt(32)
 NT = (((1,), (1,)), ((), ()))
 NEAR_FIRST = (1, 7, 2, 6, 3, 5, 4)
+FAR_FIRST = (3, 5, 4, 2, 1, 7, 6)
 
 
 def dot32(a, b):
@@ -34,11 +35,11 @@
 
 def front_kernel(
     seq_hbm, pair_hbm, wbias_hbm, wqkv_hbm, wgate_hbm, wout_hbm, wsp_hbm,
-    seq_out_ref, left_ref, right_ref,
+    sobuf, lbuf, rbuf,
     seq_v, pair_v, wbias_v, wqkv_v, wgate_v, wout_v, wsp_v,
-    seq32, zbuf, qbuf, gsend, grecv, kv, bias_v, o32, osend, orecv, m_c, l_c, mlsend, mlrecv,
-    lrsend, lbuf, rbuf, sosend, sobuf,
-    in_sem, pair_sem,
+    seq32, zbuf, qbuf, gsend, grecv, kv, bias_v, o32, osend, orecv, ml_c, mlsend, mlrecv,
+    lrsend, sosend,
+    in_sem, pair_sem, own_sem,
     z_s, z_r, q_s, q_r, g_s, g_r, a_s, kv_r, d_s, o_s, o_r, ml_s, ml_r, l_s, l_r, r_s, r_r, so_s, so_r,
 ):
     row = lax.axis_index("row")
@@ -102,7 +103,6 @@
     loads[1].wait()
     zbuf[0, 0:64] = dot32(normed, wqkv_v[1]).astype(BF16)
     zbuf[0, 64:128] = dot32(normed, wqkv_v[2]).astype(BF16)
-    qbuf[0] = dot32(normed, wqkv_v[0]).astype(BF16)
 
     pl.semaphore_wait(
         barrier, 15 + 8 - own_plane.astype(jnp.int32) + 32 - own_right.astype(jnp.int32)
@@ -126,8 +126,16 @@
     def g_copy(d):
         return col_copy(gsend.at[lax.rem(col + d, 8)], grecv.at[d], g_s, g_r, d)
 
-    for d in NEAR_FIRST:
-        z_copy(d).start()
+    turned = lax.rem(col, 2) == 1
+    late = lax.rem(col // 2, 2) == 1
+
+    def turn(k):
+        d = jnp.where(late, FAR_FIRST[k], NEAR_FIRST[k])
+        return jnp.where(turned, 8 - d, d)
+
+    for k in range(7):
+        z_copy(turn(k)).start()
+    qbuf[0] = dot32(normed, wqkv_v[0]).astype(BF16)
 
     loads[2].wait()
     gate = jax.nn.sigmoid(dot32(normed, wgate_v[...]))
@@ -161,8 +169,6 @@
         return jnp.logical_and(xh == k, col == xh * 4 + source // 2)
 
     def forward(d):
-        if d:
-            z_copy(d).wait_recv()
         for k in range(2):
             here = to_self(d, k)
 
@@ -180,10 +186,12 @@
     for e in NEAR_FIRST:
         g_copy(e).start()
     bias_rows(0)
-    for n, pair in enumerate(((1, 7), (2, 6), (3, 5), (4,))):
-        for d in pair:
-            forward(d)
-        bias_rows(n + 1)
+    for k in range(7):
+        z_copy(turn(k)).wait_recv()
+        forward(turn(k))
+        if k % 2:
+            bias_rows(k // 2 + 1)
+    bias_rows(4)
     for n in range(5, 8):
         bias_rows(n)
 
@@ -194,9 +202,10 @@
         q = h * 2 + core
         return remote(kv.at[q, c], kv.at[q, c], d_s.at[h, c], kv_r.at[q, c], partner, col)
 
-    for h in range(2):
-        @pl.loop(0, 8)
-        def _(c):
+    @pl.loop(0, 8)
+    def _(d):
+        c = lax.rem(col + 8 - d, 8)
+        for h in range(2):
             @pl.when(jnp.logical_not(jnp.logical_and(own_plane, col == c)))
             def _():
                 kv_wait(h * 2 + core, c).wait_recv()
@@ -205,18 +214,15 @@
 
     for d in range(1, 8):
         q_copy(d).wait_recv()
-    for h in range(2):
-        @pl.loop(0, 8)
-        def _(c):
-            kv_wait(h * 2 + 1 - core, c).wait_recv()
-
-    m_c[...] = jnp.zeros_like(m_c)
-    l_c[...] = jnp.ones_like(l_c)
+
+    ml_c[...] = jnp.zeros_like(ml_c)
     head_of = lane // 32
 
     @pl.loop(0, 8, unroll=4)
     def _(d):
         g = lax.rem(col + 8 - d, 8)
+        for h in range(2):
+            kv_wait(h * 2 + 1 - core, g).wait_recv()
         q = qbuf[d].astype(F32)
         q4 = jnp.concatenate([jnp.where(head_of == t, q, 0.0) for t in range(4)], axis=0).astype(BF16)
         blocks = [kv[b, g] for b in range(4)]
@@ -230,19 +236,16 @@
         total = jnp.sum(weights, axis=1, keepdims=True)
         o4 = dot32(weights.astype(BF16), values)
         out = jnp.zeros((64, 128), F32)
-        m, l = m_c[...], l_c[...]
+        ml = ml_c[...]
         for t in range(4):
             part = slice(t * 64, t * 64 + 64)
             out = jnp.where(head_of == t, o4[part], out)
-            m = jnp.where(lane == g * 4 + t, peak[part], m)
-            l = jnp.where(lane == g * 4 + t, total[part], l)
-        m_c[...] = m
-        l_c[...] = l
+            ml = jnp.where(lane == g * 4 + t, peak[part], jnp.where(lane == 32 + g * 4 + t, total[part], ml))
+        ml_c[...] = ml
         o32[:, pl.ds(pl.multiple_of(g * 8, 8), 8), :] = out.reshape(8, 8, 128)
 
     osend[...] = o32[...].astype(BF16)
-    mlsend[:, 0:8] = m_c[...].reshape(8, 8, 128)
-    mlsend[:, 8:16] = l_c[...].reshape(8, 8, 128)
+    mlsend[...] = ml_c[...].reshape(8, 8, 128)
 
     def o_copy(d):
         return col_copy(osend.at[lax.rem(col + d, 8)], orecv.at[d], o_s, o_r, d)
@@ -264,11 +267,13 @@
         ml_copy(d).wait_recv()
         o_copy(d).wait_recv()
 
-    peaks = [mlrecv[p, 0:8] for p in range(8)]
+    peaks = [mlrecv[p] for p in range(8)]
+    sums = [pltpu.roll(v, 96, 1) for v in peaks]
+    partials = [orecv[p].astype(F32) for p in range(8)]
     top = functools.reduce(jnp.maximum, peaks)
     shares = [jnp.exp(v - top) for v in peaks]
-    whole = functools.reduce(jnp.add, [s * mlrecv[p, 8:16] for p, s in enumerate(shares)])
-    share = jnp.concatenate([s / whole for s in shares], axis=0)
+    whole = functools.reduce(jnp.add, [s * v for s, v in zip(shares, sums)])
+    share = jnp.concatenate([jnp.where(lane < 32, s / whole, 0.0) for s in shares], axis=0)
     high = share.astype(BF16)
     low = (share - high.astype(F32)).astype(BF16)
     wide = dot32(high, expand) + dot32(low, expand)
@@ -276,7 +281,7 @@
     for g in range(8):
         tile = jnp.zeros((8, 128), F32)
         for p in range(8):
-            tile = tile + wide[p * 8 : p * 8 + 8, g * 128 : g * 128 + 128] * orecv[p].astype(F32)[g * 8 : g * 8 + 8]
+            tile = tile + wide[p * 8 : p * 8 + 8, g * 128 : g * 128 + 128] * partials[p][g * 8 : g * 8 + 8]
         parts.append(tile * grecv[lax.rem(col + 8 - g, 8)])
     attended = jnp.concatenate(parts, axis=1).astype(BF16)
     loads[4].wait()
@@ -284,7 +289,7 @@
     new_seq = (seq32[pl.ds(pl.multiple_of(col * 8, 8), 8), :] + update).astype(BF16).astype(F32)
     new_normed = norm_rows(new_seq).astype(BF16)
     loads[5].wait()
-    sides = dot32(new_normed, wsp_v[...]).astype(BF16).astype(F32)
+    sides = dot32(new_normed, wsp_v[...]).astype(BF16)
     lrsend[...] = sides
 
     def r_copy(n):
@@ -300,7 +305,11 @@
         return jnp.logical_and(own_right, row == n)
 
     @pl.loop(0, 32)
-    def _(n):
+    def _(j):
+        far = j // 4
+        far = 4 + (far + 1) // 2 * (1 - 2 * lax.rem(far, 2))
+        n = lax.rem(j // 2, 2) * 16 + lax.rem(z + far, 8) * 2 + lax.rem(j, 2)
+
         @pl.when(jnp.logical_not(right_here(n)))
         def _():
             r_copy(n).start()
@@ -310,12 +319,18 @@
     sosend[...] = jnp.concatenate([new_seq[:, g * 128 : g * 128 + 128] for g in range(8)], axis=0).astype(BF16)
     for d in (4, 3, 5, 2, 6, 1, 7):
         so_copy(d).start()
-    lbuf[col] = sides
-    sobuf[col] = sosend[...]
+    own = [
+        pltpu.make_async_copy(src, dst, own_sem.at[n])
+        for n, (src, dst) in enumerate(
+            ((lrsend, lbuf.at[col]), (sosend, sobuf.at[col]), (lrsend, rbuf.at[lax.rem(row, 4), col]))
+        )
+    ]
+    own[0].start()
+    own[1].start()
 
     @pl.when(own_right)
     def _():
-        rbuf[lax.rem(row, 4), col] = sides
+        own[2].start()
 
     for d in range(1, 8):
         z_copy(d).wait_send()
@@ -333,28 +348,6 @@
         def _(c):
             core_copy(h, c).wait_send()
 
-    def col_wait(buf, ss, rs, d):
-        source = lax.rem(col + 8 - d, 8)
-        return remote(buf.at[source], buf.at[source], ss.at[d], rs.at[source], row, source)
-
-    for d in range(1, 8):
-        col_wait(lbuf, l_s, l_r, d).wait_recv()
-        col_wait(sobuf, so_s, so_r, d).wait_recv()
-    left_ref[...] = lbuf[...].reshape(64, 128)
-    for c in range(8):
-        block = sobuf[c].astype(F32)
-        o32[c] = block
-    seq_out_ref[...] = jnp.concatenate(
-        [o32[:, g * 8 : g * 8 + 8, :].reshape(64, 128) for g in range(8)], axis=1
-    ).astype(BF16)
-    for q in range(4):
-        @pl.loop(0, 8)
-        def _(c):
-            @pl.when(jnp.logical_not(jnp.logical_and(own_right, jnp.logical_and(lax.rem(row, 4) == q, col == c))))
-            def _():
-                remote(rbuf.at[q, c], rbuf.at[q, c], r_s.at[0], r_r.at[q, c], partner, col).wait_recv()
-
-    right_ref[...] = rbuf[...].reshape(256, 128)
     for d in range(1, 8):
         l_copy(d).wait_send()
         so_copy(d).wait_send()
@@ -365,20 +358,42 @@
         def _():
             r_copy(n).wait_send()
 
+    own[0].wait()
+    own[1].wait()
+
+    @pl.when(own_right)
+    def _():
+        own[2].wait()
+
+    def col_wait(buf, ss, rs, d):
+        source = lax.rem(col + 8 - d, 8)
+        return remote(buf.at[source], buf.at[source], ss.at[d], rs.at[source], row, source)
+
+    for d in range(1, 8):
+        col_wait(lbuf, l_s, l_r, d).wait_recv()
+        col_wait(sobuf, so_s, so_r, d).wait_recv()
+
+    @pl.loop(0, 32)
+    def _(n):
+        q, c = n // 8, lax.rem(n, 8)
+
+        @pl.when(jnp.logical_not(jnp.logical_and(own_right, jnp.logical_and(lax.rem(row, 4) == q, col == c))))
+        def _():
+            remote(rbuf.at[q, c], rbuf.at[q, c], r_s.at[0], r_r.at[q, c], partner, col).wait_recv()
+
 
 def front(seq_state, pair_state, w_bias, w_qkv, w_gate, w_out, w_seq_pair):
     any_spec = pl.BlockSpec(memory_space=pl.ANY)
-    vmem_spec = pl.BlockSpec(memory_space=pltpu.VMEM)
     dma = pltpu.SemaphoreType.DMA
     return pl.pallas_call(
         front_kernel,
         out_shape=(
-            jax.ShapeDtypeStruct((64, 1024), BF16),
-            jax.ShapeDtypeStruct((64, 128), F32),
-            jax.ShapeDtypeStruct((256, 128), F32),
+            jax.ShapeDtypeStruct((8, 64, 128), BF16),
+            jax.ShapeDtypeStruct((8, 8, 128), BF16),
+            jax.ShapeDtypeStruct((4, 8, 8, 128), BF16),
         ),
         in_specs=[any_spec] * 7,
-        out_specs=(vmem_spec,) * 3,
+        out_specs=(any_spec,) * 3,
         scratch_shapes=[
             pltpu.VMEM((64, 1024), BF16),
             pltpu.VMEM((64, 256, 128), BF16),
@@ -398,15 +413,11 @@
             pltpu.VMEM((8, 64, 128), BF16),
             pltpu.VMEM((8, 64, 128), BF16),
             pltpu.VMEM((64, 128), F32),
-            pltpu.VMEM((64, 128), F32),
-            pltpu.VMEM((8, 16, 128), F32),
-            pltpu.VMEM((8, 16, 128), F32),
-            pltpu.VMEM((8, 128), F32),
             pltpu.VMEM((8, 8, 128), F32),
-            pltpu.VMEM((4, 8, 8, 128), F32),
+            pltpu.VMEM((8, 8, 128), F32),
+            pltpu.VMEM((8, 128), BF16),
             pltpu.VMEM((64, 128), BF16),
-            pltpu.VMEM((8, 64, 128), BF16),
-            dma((6,)), dma((8,)),
+            dma((6,)), dma((8,)), dma((3,)),
             dma((8,)), dma((8,)), dma((8,)), dma((8,)), dma((8,)), dma((8,)),
             dma((8, 2)), dma((4, 8)), dma((2, 8)),
             dma((8,)), dma((8,)), dma((8,)), dma((8,)), dma((8,)), dma((8,)),
@@ -419,7 +430,7 @@
     )(seq_state, pair_state, w_bias, w_qkv, w_gate, w_out, w_seq_pair)
 
 
-def pair_kernel(x_ref, left_ref, right_ref, wp_ref, wu_ref, wd_ref, o_ref, mix_ref, right2_ref):
+def pair_kernel(x_ref, left_ref, right_ref, wp_ref, wu_ref, wd_ref, seq_ref, o_ref, seq_out_ref, mix_ref, right2_ref):
     @pl.when(pl.program_id(0) == 0)
     def _():
         w = wp_ref[...].astype(F32)
@@ -431,59 +442,83 @@
         mix_ref[0:128, 128:256] = eye.astype(BF16)
         mix_ref[128:256, 0:128] = centred.astype(BF16)
         mix_ref[128:256, 128:256] = wp_ref[...]
-        r = right_ref[:, 64:128]
-        right2_ref[...] = jnp.concatenate([r, r], axis=1)
+        r = right_ref[...].astype(F32).reshape(256, 128)[:, 64:128]
+        right2_ref[...] = jnp.concatenate([r, r], axis=1).astype(BF16)
+        rows = seq_ref[...].astype(F32)
+        seq_out_ref[...] = jnp.concatenate(
+            [rows[:, g * 8 : g * 8 + 8, :].reshape(64, 128) for g in range(8)], axis=1
+        ).astype(BF16)
 
     lane = lax.broadcasted_iota(jnp.int32, (1, 128), 1)
-    for start in range(0, PAIR_ROWS, PAIR_CHUNK):
+
+    lefts = left_ref[...].astype(F32).reshape(PAIR_ROWS, 128)
+
+    def update(start):
         features, rows = [], []
         for i in range(start, start + PAIR_CHUNK):
-            left = left_ref[pl.ds(i, 1), 0:64]
+            left = lefts[i : i + 1, 0:64]
             left2 = jnp.concatenate([left, left], axis=1)
-            scale = jnp.where(lane < 64, left2, -1.0)
-            shift = jnp.where(lane < 64, 0.0, left2)
-            features.append((right2_ref[...] * scale + shift).astype(BF16))
+            scale = jnp.where(lane < 64, left2, -1.0).astype(BF16)
+            shift = jnp.where(lane < 64, 0.0, left2).astype(BF16)
+            features.append(right2_ref[...] * scale + shift)
             rows.append(x_ref[i])
         mixed = dot32(
             jnp.concatenate([jnp.concatenate(rows, axis=0), jnp.concatenate(features, axis=0)], axis=1),
             mix_ref[...],
         )
-        centred, updated = mixed[:, :128], mixed[:, 128:]
+        return mixed[:, :128], mixed[:, 128:]
+
+    def normed(centred):
         variance = jnp.mean(centred * centred, axis=1, keepdims=True)
-        normed = (centred * lax.rsqrt(variance + EPSILON)).astype(BF16)
-        hidden = jnp.maximum(dot32(normed, wu_ref[...]), 0.0).astype(BF16)
+        return (centred * lax.rsqrt(variance + EPSILON)).astype(BF16)
+
+    def finish(start, hidden, updated):
         result = (updated + dot32(hidden, wd_ref[...])).astype(BF16)
         for i in range(PAIR_CHUNK):
             o_ref[start + i] = result[i * 256 : (i + 1) * 256]
 
-
-def pair_transition(x, left, right, wp, wu, wd):
+    count = PAIR_ROWS // PAIR_CHUNK
+    ready, updates, hidden = {}, {}, {}
+    for t in range(count + 2):
+        if t < count:
+            centred, updates[t] = update(t * PAIR_CHUNK)
+        if 0 <= t - 1 < count:
+            hidden[t - 1] = jnp.maximum(dot32(ready[t - 1], wu_ref[...]).astype(BF16), 0)
+        if t < count:
+            ready[t] = normed(centred)
+        if 0 <= t - 2:
+            finish((t - 2) * PAIR_CHUNK, hidden[t - 2], updates[t - 2])
+
+
+def pair_transition(x, left, right, wp, wu, wd, seq):
     rows = x.shape[0]
 
-    def whole(array):
-        return pl.BlockSpec(array.shape, lambda i: (0,) * array.ndim)
+    def whole(shape):
+        return pl.BlockSpec(shape, lambda i: (0,) * len(shape))
 
     return pl.pallas_call(
         pair_kernel,
         grid=(rows // PAIR_ROWS,),
-        out_shape=jax.ShapeDtypeStruct(x.shape, BF16),
+        out_shape=(jax.ShapeDtypeStruct(x.shape, BF16), jax.ShapeDtypeStruct((64, 1024), BF16)),
         in_specs=[
             pl.BlockSpec((PAIR_ROWS, 256, 128), lambda i: (i, 0, 0)),
-            pl.BlockSpec((PAIR_ROWS, 128), lambda i: (i, 0)),
-            whole(right),
-            whole(wp),
-            whole(wu),
-            whole(wd),
+            pl.BlockSpec((PAIR_ROWS // 8, 8, 128), lambda i: (i, 0, 0)),
+            whole(right.shape),
+            whole(wp.shape),
+            whole(wu.shape),
+            whole(wd.shape),
+            whole(seq.shape),
         ],
-        out_specs=pl.BlockSpec((PAIR_ROWS, 256, 128), lambda i: (i, 0, 0)),
-        scratch_shapes=[pltpu.VMEM((256, 256), BF16), pltpu.VMEM((256, 128), F32)],
+        out_specs=(pl.BlockSpec((PAIR_ROWS, 256, 128), lambda i: (i, 0, 0)), whole((64, 1024))),
+        scratch_shapes=[pltpu.VMEM((256, 256), BF16), pltpu.VMEM((256, 128), BF16)],
         compiler_params=pltpu.CompilerParams(dimension_semantics=("arbitrary",)),
-    )(x, left, right, wp, wu, wd)
+    )(x, left, right, wp, wu, wd, seq)
 
 
 def body(seq_state, pair_state, w_bias, w_qkv, w_gate, w_out, w_seq_pair, w_pair_out, w_up, w_down):
-    seq_out, left, right = front(seq_state, pair_state, w_bias.T, w_qkv, w_gate, w_out, w_seq_pair)
-    return (seq_out, pair_transition(pair_state, left, right, w_pair_out, w_up, w_down))
+    seq_rows, left, right = front(seq_state, pair_state, w_bias.T, w_qkv, w_gate, w_out, w_seq_pair)
+    pair_out, seq_out = pair_transition(pair_state, left, right, w_pair_out, w_up, w_down, seq_rows)
+    return (seq_out, pair_out)
 
 
 def solution(mesh):

time: 61.9 us -> 59.1 us (0.955)
  Pallas kernels: 60.1 us -> 57.9 us
  local copies, waits for them, and re-layouts: 0.66 us -> 0 us
    pallas_call x2, Pallas kernels: 60.1 us -> 57.9 us  [the longest x1 43.5 us: front(): pl.pallas_call(front_kernel, out_shape=(jax.ShapeDtypeStruct((8, 64, 128)...]
    unnamed x3 -> x0, local copies, waits for them, and re-layouts: 0.66 us -> none
where the time goes in v4:
time: 59.1 us; the launch traced here: 58.5 us
  Pallas kernels  57.9 us (98%)
  between operations  0.64 us (1%)
    pallas_call x1, Pallas kernels, front(): pl.pallas_call(front_kernel, out_shape=(jax.ShapeDtypeStruct((8, 64, 128)...  43.5 us
    pallas_call x1, Pallas kernels, pair_transition(): pl.pallas_call(pair_kernel, grid=(rows // PAIR_ROWS,), out_shape=(jax.Sha...  14.4 us

profile of v4, /device:TPU:1, one launch (start us, length us, event | category | flops | bytes accessed | tf_op | source)
XLA Modules:
  0.0 58.5 jit_solution(9977724889212080749)
XLA Ops:
  0.6 43.5 %shard_map.113 = (bf16[8,64,128]{2,1,0:T(8,128)(2,1)}, bf16[8,8,128]{2,1,0:T(8,128)(2,1)}, bf16[4,8,8,128]{3,2,1,0:T(8,128)(2,1)}) custom-call(bf16[64,1024]{1,0:T(8,128)(2,1)} %seq_hbm.1, bf16[64,256,128]{2,1,0:T(8,128)(2,1)} %x_ref.1, bf16[32,128]{1,0:T(8,128)(2,1)} %bitcast.1, bf16[3,1024,128]{2,1,0:T(8,128)(2,1)} %wqkv_hbm.1, ...), custom_call_target="tpu_custom_call" | custom-call | flops 3000000000 | bytes 8000000 | tf_op jit(solution)/shard_map/pallas_call | solution.py:388
  44.1 14.4 %shard_map.114 = (bf16[64,256,128]{2,1,0:T(8,128)(2,1)}, bf16[64,1024]{1,0:T(8,128)(2,1)}) custom-call(bf16[64,256,128]{2,1,0:T(8,128)(2,1)} %x_ref.1, bf16[8,8,128]{2,1,0:T(8,128)(2,1)} %get-tuple-element.7.left_ref, bf16[4,8,8,128]{3,2,1,0:T(8,128)(2,1)} %get-tuple-element.8.right_ref, bf16[128,128]{1,0:T(8,128)(2,1)} %wp_ref.1, bf16[128,512]{1,0:T(8,128)(2,1)} %wu_ref.1, ...), custom_call_target="tpu_custom_call" | custom-call | tf_op jit(solution)/shard_map/pallas_call | solution.py:499

commit v5 on v4

--- a/solution.py
+++ b/solution.py
@@ -79,21 +79,8 @@
         def _():
             greet(plane_row, c)
 
-    @pl.loop(0, 32)
-    def _(n):
-        r, c = 4 * col + n // 8, lax.rem(n, 8)
-
-        @pl.when(jnp.logical_not(jnp.logical_and(own_right, jnp.logical_and(row == r, col == c))))
-        def _():
-            greet(r, c)
-
     def pair_load(n):
         return pltpu.make_async_copy(pair_hbm.at[pl.ds(n * 8, 8)], pair_v.at[pl.ds(n * 8, 8)], pair_sem.at[n])
-
-    for n in range(8):
-        pair_load(n).start()
-    for n in (4, 5):
-        loads[n].start()
 
     lane = lax.broadcasted_iota(jnp.int32, (1, 128), 1)
     loads[0].wait()
@@ -101,12 +88,14 @@
     seq32[...] = x
     normed = norm_rows(x).astype(BF16)
     loads[1].wait()
+    for n in range(8):
+        pair_load(n).start()
+    for n in (4, 5):
+        loads[n].start()
     zbuf[0, 0:64] = dot32(normed, wqkv_v[1]).astype(BF16)
     zbuf[0, 64:128] = dot32(normed, wqkv_v[2]).astype(BF16)
 
-    pl.semaphore_wait(
-        barrier, 15 + 8 - own_plane.astype(jnp.int32) + 32 - own_right.astype(jnp.int32)
-    )
+    pl.semaphore_wait(barrier, 15 + 8 - own_plane.astype(jnp.int32))
 
     def remote(src, dst, ss, rs, r, c):
         return pltpu.make_async_remote_copy(
@@ -130,11 +119,17 @@
     late = lax.rem(col // 2, 2) == 1
 
     def turn(k):
-        d = jnp.where(late, FAR_FIRST[k], NEAR_FIRST[k])
+        near, far = NEAR_FIRST[6], FAR_FIRST[6]
+        for n in range(6):
+            near = jnp.where(k == n, NEAR_FIRST[n], near)
+            far = jnp.where(k == n, FAR_FIRST[n], far)
+        d = jnp.where(late, far, near)
         return jnp.where(turned, 8 - d, d)
 
-    for k in range(7):
+    @pl.loop(0, 7)
+    def _(k):
         z_copy(turn(k)).start()
+
     qbuf[0] = dot32(normed, wqkv_v[0]).astype(BF16)
 
     loads[2].wait()
@@ -149,7 +144,7 @@
 
     def bias_rows(n):
         pair_load(n).wait()
-        c = dot32(pair_v[n * 8 : n * 8 + 8].reshape(2048, 128), centre)
+        c = dot32(pair_v[pl.ds(n * 8, 8)].reshape(2048, 128), centre)
         variance = jnp.mean(c * c, axis=1, keepdims=True)
         b = dot_nt(wb_t, (c * lax.rsqrt(variance + EPSILON)).astype(BF16)).astype(BF16).astype(F32)
         for i in range(8):
@@ -181,19 +176,21 @@
                 plane_copy(d, k).start()
 
     forward(0)
-    for e in NEAR_FIRST:
-        q_copy(e).start()
-    for e in NEAR_FIRST:
-        g_copy(e).start()
-    bias_rows(0)
-    for k in range(7):
-        z_copy(turn(k)).wait_recv()
-        forward(turn(k))
-        if k % 2:
-            bias_rows(k // 2 + 1)
-    bias_rows(4)
-    for n in range(5, 8):
+    @pl.loop(1, 8)
+    def _(d):
+        q_copy(d).start()
+        g_copy(d).start()
+
+    @pl.loop(0, 8)
+    def _(n):
         bias_rows(n)
+        for half in range(2):
+            k = n * 2 + half
+
+            @pl.when(k < 7)
+            def _():
+                z_copy(turn(k)).wait_recv()
+                forward(turn(k))
 
     def kv_wait(q, c):
         return remote(kv.at[q, c], kv.at[q, c], d_s.at[0, 0], kv_r.at[q, c], partner, col)
@@ -212,8 +209,10 @@
 
             core_copy(h, c).start()
 
-    for d in range(1, 8):
+    @pl.loop(1, 8)
+    def _(d):
         q_copy(d).wait_recv()
+
 
     ml_c[...] = jnp.zeros_like(ml_c)
     head_of = lane // 32
@@ -253,16 +252,19 @@
     def ml_copy(d):
         return col_copy(mlsend.at[lax.rem(col + d, 8)], mlrecv.at[d], ml_s, ml_r, d)
 
-    for d in (4, 3, 5, 2, 6, 1, 7):
+    @pl.loop(1, 8)
+    def _(d):
         ml_copy(d).start()
         o_copy(d).start()
+
     orecv[0] = osend[col]
     mlrecv[0] = mlsend[col]
     grecv[0] = gsend[col]
     ea = lax.broadcasted_iota(jnp.int32, (128, 1024), 0)
     eb = lax.broadcasted_iota(jnp.int32, (128, 1024), 1)
     expand = jnp.where(ea == eb // 32, 1.0, 0.0).astype(BF16)
-    for d in range(1, 8):
+    @pl.loop(1, 8)
+    def _(d):
         g_copy(d).wait_recv()
         ml_copy(d).wait_recv()
         o_copy(d).wait_recv()
@@ -314,11 +316,16 @@
         def _():
             r_copy(n).start()
 
-    for d in (4, 3, 5, 2, 6, 1, 7):
+    @pl.loop(1, 8)
+    def _(d):
         l_copy(d).start()
+
     sosend[...] = jnp.concatenate([new_seq[:, g * 128 : g * 128 + 128] for g in range(8)], axis=0).astype(BF16)
-    for d in (4, 3, 5, 2, 6, 1, 7):
+
+    @pl.loop(1, 8)
+    def _(d):
         so_copy(d).start()
+
     own = [
         pltpu.make_async_copy(src, dst, own_sem.at[n])
         for n, (src, dst) in enumerate(
@@ -332,23 +339,28 @@
     def _():
         own[2].start()
 
-    for d in range(1, 8):
+    @pl.loop(1, 8)
+    def _(d):
         z_copy(d).wait_send()
         q_copy(d).wait_send()
         g_copy(d).wait_send()
         ml_copy(d).wait_send()
         o_copy(d).wait_send()
-    for d in range(8):
+
+    @pl.loop(0, 8)
+    def _(d):
         for k in range(2):
             @pl.when(jnp.logical_not(to_self(d, k)))
             def _():
                 plane_copy(d, k).wait_send()
+
     for h in range(2):
         @pl.loop(0, 8)
         def _(c):
             core_copy(h, c).wait_send()
 
-    for d in range(1, 8):
+    @pl.loop(1, 8)
+    def _(d):
         l_copy(d).wait_send()
         so_copy(d).wait_send()
 
@@ -369,7 +381,8 @@
         source = lax.rem(col + 8 - d, 8)
         return remote(buf.at[source], buf.at[source], ss.at[d], rs.at[source], row, source)
 
-    for d in range(1, 8):
+    @pl.loop(1, 8)
+    def _(d):
         col_wait(lbuf, l_s, l_r, d).wait_recv()
         col_wait(sobuf, so_s, so_r, d).wait_recv()
 

time: 59.1 us -> 56.3 us (0.953)
  Pallas kernels: 57.9 us -> 55.5 us
    pallas_call x1, Pallas kernels: 43.5 us -> 41.1 us  [front(): pl.pallas_call(front_kernel, out_shape=(jax.ShapeDtypeStruct((8, 64, 128)...]
where the time goes in v5:
time: 56.3 us; the launch traced here: 56.1 us
  Pallas kernels  55.5 us (99%)
  between operations  0.64 us (1%)
    pallas_call x1, Pallas kernels, front(): pl.pallas_call(front_kernel, out_shape=(jax.ShapeDtypeStruct((8, 64, 128)...  41.1 us
    pallas_call x1, Pallas kernels, pair_transition(): pl.pallas_call(pair_kernel, grid=(rows // PAIR_ROWS,), out_shape=(jax.Sha...  14.4 us

profile of v5, /device:TPU:1, one launch (start us, length us, event | category | flops | bytes accessed | tf_op | source)
XLA Modules:
  0.0 56.1 jit_solution(14778892801552084124)
XLA Ops:
  0.6 41.1 %shard_map.113 = (bf16[8,64,128]{2,1,0:T(8,128)(2,1)}, bf16[8,8,128]{2,1,0:T(8,128)(2,1)}, bf16[4,8,8,128]{3,2,1,0:T(8,128)(2,1)}) custom-call(bf16[64,1024]{1,0:T(8,128)(2,1)} %seq_hbm.1, bf16[64,256,128]{2,1,0:T(8,128)(2,1)} %x_ref.1, bf16[32,128]{1,0:T(8,128)(2,1)} %bitcast.1, bf16[3,1024,128]{2,1,0:T(8,128)(2,1)} %wqkv_hbm.1, ...), custom_call_target="tpu_custom_call" | custom-call | flops 3000000000 | bytes 8000000 | tf_op jit(solution)/shard_map/pallas_call | solution.py:401
  41.8 14.4 %shard_map.114 = (bf16[64,256,128]{2,1,0:T(8,128)(2,1)}, bf16[64,1024]{1,0:T(8,128)(2,1)}) custom-call(bf16[64,256,128]{2,1,0:T(8,128)(2,1)} %x_ref.1, bf16[8,8,128]{2,1,0:T(8,128)(2,1)} %get-tuple-element.7.left_ref, bf16[4,8,8,128]{3,2,1,0:T(8,128)(2,1)} %get-tuple-element.8.right_ref, bf16[128,128]{1,0:T(8,128)(2,1)} %wp_ref.1, bf16[128,512]{1,0:T(8,128)(2,1)} %wu_ref.1, ...), custom_call_target="tpu_custom_call" | custom-call | tf_op jit(solution)/shard_map/pallas_call | solution.py:512

commit v6 on v5

--- a/solution.py
+++ b/solution.py
@@ -54,11 +54,11 @@
     loads = [
         pltpu.make_async_copy(src, dst, in_sem.at[n])
         for n, (src, dst) in enumerate(
-            ((seq_hbm, seq_v), (wqkv_hbm, wqkv_v), (wgate_hbm, wgate_v), (wbias_hbm, wbias_v),
-             (wout_hbm, wout_v), (wsp_hbm, wsp_v))
+            ((seq_hbm, seq_v), (wqkv_hbm.at[pl.ds(1, 2)], wqkv_v.at[pl.ds(1, 2)]), (wgate_hbm, wgate_v),
+             (wbias_hbm, wbias_v), (wout_hbm, wout_v), (wsp_hbm, wsp_v), (wqkv_hbm.at[0], wqkv_v.at[0]))
         )
     ]
-    for n in range(4):
+    for n in (0, 1, 6, 2, 3):
         loads[n].start()
 
     barrier = pltpu.get_barrier_semaphore()
@@ -130,11 +130,6 @@
     def _(k):
         z_copy(turn(k)).start()
 
-    qbuf[0] = dot32(normed, wqkv_v[0]).astype(BF16)
-
-    loads[2].wait()
-    gate = jax.nn.sigmoid(dot32(normed, wgate_v[...]))
-    gsend[...] = gate.reshape(8, 8, 128)
 
     loads[3].wait()
     wb_t = wbias_v[...]
@@ -176,9 +171,19 @@
                 plane_copy(d, k).start()
 
     forward(0)
+    loads[6].wait()
+    qbuf[0] = dot32(normed, wqkv_v[0]).astype(BF16)
+
     @pl.loop(1, 8)
     def _(d):
         q_copy(d).start()
+
+    loads[2].wait()
+    gate = jax.nn.sigmoid(dot32(normed, wgate_v[...]))
+    gsend[...] = gate.reshape(8, 8, 128)
+
+    @pl.loop(1, 8)
+    def _(d):
         g_copy(d).start()
 
     @pl.loop(0, 8)
@@ -430,7 +435,7 @@
             pltpu.VMEM((8, 8, 128), F32),
             pltpu.VMEM((8, 128), BF16),
             pltpu.VMEM((64, 128), BF16),
-            dma((6,)), dma((8,)), dma((3,)),
+            dma((7,)), dma((8,)), dma((3,)),
             dma((8,)), dma((8,)), dma((8,)), dma((8,)), dma((8,)), dma((8,)),
             dma((8, 2)), dma((4, 8)), dma((2, 8)),
             dma((8,)), dma((8,)), dma((8,)), dma((8,)), dma((8,)), dma((8,)),
@@ -457,13 +462,13 @@
         mix_ref[128:256, 128:256] = wp_ref[...]
         r = right_ref[...].astype(F32).reshape(256, 128)[:, 64:128]
         right2_ref[...] = jnp.concatenate([r, r], axis=1).astype(BF16)
-        rows = seq_ref[...].astype(F32)
-        seq_out_ref[...] = jnp.concatenate(
-            [rows[:, g * 8 : g * 8 + 8, :].reshape(64, 128) for g in range(8)], axis=1
-        ).astype(BF16)
 
     lane = lax.broadcasted_iota(jnp.int32, (1, 128), 1)
 
+    seq = seq_ref[...].astype(F32)
+    seq_out_ref[...] = jnp.concatenate(
+        [seq[:, g * 8 : g * 8 + 8, :].reshape(PAIR_ROWS, 128) for g in range(8)], axis=1
+    ).astype(BF16)
     lefts = left_ref[...].astype(F32).reshape(PAIR_ROWS, 128)
 
     def update(start):
@@ -520,9 +525,9 @@
             whole(wp.shape),
             whole(wu.shape),
             whole(wd.shape),
-            whole(seq.shape),
+            pl.BlockSpec((PAIR_ROWS // 8, 64, 128), lambda i: (i, 0, 0)),
         ],
-        out_specs=(pl.BlockSpec((PAIR_ROWS, 256, 128), lambda i: (i, 0, 0)), whole((64, 1024))),
+        out_specs=(pl.BlockSpec((PAIR_ROWS, 256, 128), lambda i: (i, 0, 0)), pl.BlockSpec((PAIR_ROWS, 1024), lambda i: (i, 0))),
         scratch_shapes=[pltpu.VMEM((256, 256), BF16), pltpu.VMEM((256, 128), BF16)],
         compiler_params=pltpu.CompilerParams(dimension_semantics=("arbitrary",)),
     )(x, left, right, wp, wu, wd, seq)

time: 56.3 us -> 56.3 us (level)
  no operation moved by 1% of the time
where the time goes in v6:
time: 56.3 us; the launch traced here: 56.2 us
  Pallas kernels  55.5 us (99%)
  between operations  0.64 us (1%)
    pallas_call x1, Pallas kernels, front(): pl.pallas_call(front_kernel, out_shape=(jax.ShapeDtypeStruct((8, 64, 128)...  41.1 us
    pallas_call x1, Pallas kernels, pair_transition(): pl.pallas_call(pair_kernel, grid=(rows // PAIR_ROWS,), out_shape=(jax.Sha...  14.4 us

profile of v6, /device:TPU:1, one launch (start us, length us, event | category | flops | bytes accessed | tf_op | source)
XLA Modules:
  0.0 56.2 jit_solution(6791457290505917998)
XLA Ops:
  0.6 41.1 %shard_map.113 = (bf16[8,64,128]{2,1,0:T(8,128)(2,1)}, bf16[8,8,128]{2,1,0:T(8,128)(2,1)}, bf16[4,8,8,128]{3,2,1,0:T(8,128)(2,1)}) custom-call(bf16[64,1024]{1,0:T(8,128)(2,1)} %seq_hbm.1, bf16[64,256,128]{2,1,0:T(8,128)(2,1)} %x_ref.1, bf16[32,128]{1,0:T(8,128)(2,1)} %bitcast.1, bf16[3,1024,128]{2,1,0:T(8,128)(2,1)} %wqkv_hbm.1, ...), custom_call_target="tpu_custom_call" | custom-call | flops 3000000000 | bytes 8000000 | tf_op jit(solution)/shard_map/pallas_call | solution.py:406
  41.8 14.4 %shard_map.114 = (bf16[64,256,128]{2,1,0:T(8,128)(2,1)}, bf16[64,1024]{1,0:T(8,128)(2,1)}) custom-call(bf16[64,256,128]{2,1,0:T(8,128)(2,1)} %x_ref.1, bf16[8,8,128]{2,1,0:T(8,128)(2,1)} %get-tuple-element.7.left_ref, bf16[4,8,8,128]{3,2,1,0:T(8,128)(2,1)} %get-tuple-element.8.right_ref, bf16[128,128]{1,0:T(8,128)(2,1)} %wp_ref.1, bf16[128,512]{1,0:T(8,128)(2,1)} %wu_ref.1, ...), custom_call_target="tpu_custom_call" | custom-call | tf_op jit(solution)/shard_map/pallas_call | solution.py:517
